TPU v7x, 128 devices: a whole 4x4x4 slice. The times are simulated.
128 devices in a mesh: blk: 64 (over x_lo, y, z, core), tensor: 2 (over x_hi).
Axes of the slice: x: 4 (x_hi: 2, x_lo: 2; x = x_hi * 2 + x_lo), y: 4, z: 4, core: 2. Of those that a mesh axis runs over, the one named last changes fastest.
Arguments:
- tokens: bfloat16 [256, 8192], P('blk'), may hold values from -6 to 6
- gate_weight: bfloat16 [29568, 8192], P(('blk', 'tensor')), may hold values from -0.0625 to 0.0625
- up_weight: bfloat16 [29568, 8192], P(('blk', 'tensor')), may hold values from -0.0625 to 0.0625
- down_weight: bfloat16 [29568, 8192], P(('blk', 'tensor')), may hold values from -0.03125 to 0.03125
Outputs:
- mixed: bfloat16 [256, 8192], P(('blk', 'tensor'))
All inputs are finite; a program needn't handle non-finite values.
Results may differ from a plain program's by a relative error of at most 0.009.
Values may be sent and summed in bfloat16 or wider, within the bound.
No kernel may reach another device: no remote copies, remote signals or barrier semaphores. Data moves between devices by JAX's collectives and lax.ppermute only.
A program may use at most 64 MiB of HBM per device.

v0:
```python
import jax
import jax.numpy as jnp
from jax import lax
from jax.sharding import PartitionSpec as P


def project_rows(left, weight):
    return lax.dot_general(
        left, weight, (((1,), (1,)), ((), ())), preferred_element_type=jnp.float32
    )


def per_device(tokens, gate_weight, up_weight, down_weight):
    piece = lax.all_gather(tokens, "blk", axis=0, tiled=True)
    gate = project_rows(piece, gate_weight)
    up_part = project_rows(piece, up_weight)
    hidden = (jax.nn.silu(gate) * up_part).astype(jnp.bfloat16)
    total = lax.psum_scatter(
        jnp.dot(hidden, down_weight, preferred_element_type=jnp.float32),
        ("blk", "tensor"),
        scatter_dimension=0,
        tiled=True,
    )
    return total.astype(jnp.bfloat16)


def solution(mesh):
    placed = (
        P("blk", None),
        P(("blk", "tensor"), None),
        P(("blk", "tensor"), None),
        P(("blk", "tensor"), None),
    )
    return jax.shard_map(
        per_device,
        mesh=mesh,
        in_specs=placed,
        out_specs=P(("blk", "tensor"), None),
        check_vma=False,
    )
```

profile of v0, /device:TPU:0, one launch (start us, length us, event | category | flops | bytes accessed | tf_op | source)
XLA Modules:
  0.0 261.2 jit_solution(18180911876720562141)
XLA Ops:
  6.5 0.0 all-gather.3.cloned.1.call-start
  6.5 0.7 all-gather.3.cloned.1.call-update
  7.3 109.7 %all-gather.3.cloned.1.call-done = bf16[64,4,8192]{2,1,0:T(4,128)(2,1)} async-done(((bf16[1,4,8192]{2,1,0:T(4,128)(2,1)}), bf16[64,4,8192]{2,1,0:T(4,128)(2,1)}) %all-gather.3.cloned.1.call-update) | async-done | bytes 4194320 | tf_op jit(solution)/shard_map/all_gather | solution.py:14
  116.9 6.9 %reshape.1 = bf16[256,8192]{1,0:T(8,128)(2,1)} reshape(bf16[64,4,8192]{2,1,0:T(4,128)(2,1)} %all-gather.3.cloned.1.call-done) | data formatting | bytes 8388608
  123.9 4.7 %fusion.9 = f32[256,231]{0,1:T(8,128)S(1)} fusion(bf16[256,8192]{1,0:T(8,128)(2,1)} %reshape.1, bf16[231,8192]{1,0:T(8,128)(2,1)} %param.5), kind=kOutput, calls=%fused_computation.11 | convolution fusion | flops 968884224 | bytes 8215552 | tf_op jit(solution)/shard_map/dot_general | solution.py:8
  128.6 12.3 %fusion.1 = f32[256,8192]{1,0:T(8,128)} fusion(bf16[231,8192]{1,0:T(8,128)(2,1)} %param.7, bf16[256,8192]{1,0:T(8,128)(2,1)} %reshape.1, bf16[231,8192]{1,0:T(8,128)(2,1)} %param.6, f32[256,231]{0,1:T(8,128)S(1)} %fusion.9), kind=kOutput, calls=%fused_computation.2 | convolution fusion | flops 1938123264 | bytes 20388864 | tf_op jit(solution)/shard_map/dot_general | solution.py:19
  140.9 111.9 %all-reduce.2 = bf16[256,8192]{1,0:T(8,128)(2,1)} all-reduce(f32[256,8192]{1,0:T(8,128)} %fusion.1), channel_id=2, replica_groups=mesh['blk'=64,'tensor'=2] {'blk','tensor'}, use_global_device_ids=true, to_apply=%region_0.1.clone | all-reduce | flops 2097152 | bytes 12582912
  252.8 1.6 dynamic-slice_convert_fusion
Async XLA Ops:
  6.5 110.4 %all-gather.3.cloned.1.call-start = ((), (), s32[]{:S(2)}) async-start(), calls=%async_computation | async-start | bytes 4259840 | tf_op jit(solution)/shard_map/all_gather | solution.py:14
Sparse Core Ops, SparseCore 0:
  9.0 107.8 all-gather.2
where the time goes:
time: 262 us; the launch traced here: 261 us
  blocking collectives  112 us (43%)
  waiting for transfers between devices  110 us (42%)
  matrix products  17.1 us (7%)
  between operations  13.4 us (5%)
  local copies, waits for them, and re-layouts  8.48 us (3%)
    unnamed x1, blocking collectives  112 us
    all_gather x1, waiting for transfers between devices, per_device(): piece = lax.all_gather(tokens, 'blk', axis=0, tiled=True)  110 us
    dot_general x1, matrix products, per_device(): jnp.dot(hidden, down_weight, preferred_element_type=jnp.float32)  12.3 us
    unnamed x1, local copies, waits for them, and re-layouts  6.92 us
  transfers between devices with their start and end apart: 1, of which 1 were waited for; matrix products, arithmetic and copies ran while one was open for 0% of the time, Pallas kernels for 0%

commit v1 on v0

v1 whole, which is shorter than its diff:
```python
import jax
import jax.numpy as jnp
from jax import lax
from jax.sharding import Mesh, PartitionSpec as P

ALL = ("xl", "y", "z", "c", "xh")
CHIPS = ("xl", "y", "z")
BF = jnp.bfloat16
F32 = jnp.float32


def flat(xl, y, z, c, xh):
    return (((xl * 4 + y) * 4 + z) * 2 + c) * 2 + xh


def every():
    for xl in range(2):
        for y in range(4):
            for z in range(4):
                for c in range(2):
                    for xh in range(2):
                        yield xl, y, z, c, xh


def swap_core(v):
    pairs = [(flat(a, y, z, c, h), flat(a, y, z, 1 - c, h)) for a, y, z, c, h in every()]
    return lax.ppermute(v, ALL, pairs)


def swap_far(v):
    pairs = [(flat(a, y, z, c, h), flat(a, y, z, c, 1 - h)) for a, y, z, c, h in every()]
    return lax.ppermute(v, ALL, pairs)


def rows_of(left, weight):
    return lax.dot_general(
        left, weight, (((1,), (1,)), ((), ())), preferred_element_type=F32
    )


def per_device(tokens, gate_weight, up_weight, down_weight):
    d = tokens.shape[1]
    half = d // 2
    c = lax.axis_index("c")
    h = lax.axis_index("xh")
    lo, hi = tokens[:, :half], tokens[:, half:]
    mine = jnp.where(c == 0, lo, hi)
    other = jnp.where(c == 0, hi, lo)
    with jax.named_scope("pre"):
        got = swap_core(other)
    eight = jnp.where(c == 0, jnp.concatenate([mine, got]), jnp.concatenate([got, mine]))
    with jax.named_scope("gather"):
        x_mine = lax.all_to_all(
            jnp.broadcast_to(eight[None], (32, 8, half)), CHIPS, 0, 0, tiled=True
        ).reshape(256, half)
    with jax.named_scope("share"):
        x_got = swap_core(x_mine)
    x = jnp.where(
        c == 0,
        jnp.concatenate([x_mine, x_got], 1),
        jnp.concatenate([x_got, x_mine], 1),
    )
    gate = rows_of(x, gate_weight)
    up = rows_of(x, up_weight)
    hidden = (jax.nn.silu(gate) * up).astype(BF)
    part = jnp.dot(hidden, down_weight, preferred_element_type=F32)
    p_mine = jnp.where(c == 0, part[:, :half], part[:, half:])
    p_other = jnp.where(c == 0, part[:, half:], part[:, :half]).astype(BF)
    with jax.named_scope("fold"):
        p_got = swap_core(p_other)
    total = (p_mine + p_got.astype(F32)).astype(BF)
    with jax.named_scope("scatter"):
        pieces = lax.all_to_all(total.reshape(32, 8, half), CHIPS, 0, 0, tiled=True)
    total = jnp.sum(pieces.astype(F32), axis=0).reshape(2, 2, 2, half)
    keep = jnp.where(h == 0, total[:, 0], total[:, 1])
    send = jnp.where(h == 0, total[:, 1], total[:, 0]).astype(BF)
    with jax.named_scope("far"):
        keep = keep + swap_far(send).astype(F32)
    keep = keep.astype(BF)
    own = jnp.where(c == 0, keep[0], keep[1])
    away = jnp.where(c == 0, keep[1], keep[0])
    with jax.named_scope("post"):
        back = swap_core(away)
    return jnp.where(
        c == 0,
        jnp.concatenate([own, back], 1),
        jnp.concatenate([back, own], 1),
    )


def solution(mesh):
    fine = Mesh(mesh.devices.reshape(2, 4, 4, 2, 2), ALL)
    blk = ("xl", "y", "z", "c")
    return jax.shard_map(
        per_device,
        mesh=fine,
        in_specs=(P(blk, None), P(ALL, None), P(ALL, None), P(ALL, None)),
        out_specs=P(ALL, None),
        check_vma=False,
    )
```

time: 262 us -> 99 us (0.38)
  blocking collectives: 112 us -> 37 us
  waiting for transfers between devices: 110 us -> 42.2 us
  between operations: 13.4 us -> 0.12 us
  matrix products: 17.1 us -> 4.27 us
  starting transfers between devices: 0.01 us -> 8.23 us
  local copies, waits for them, and re-layouts: 8.48 us -> 1.05 us
  other arithmetic: 0 us -> 4.75 us
    unnamed x1 -> x0, blocking collectives: 112 us -> none
    all_gather x1 -> x0, waiting for transfers between devices: 110 us -> none  [per_device(): piece = lax.all_gather(tokens, 'blk', axis=0, tiled=True)]
    all_to_all x0 -> x1, blocking collectives: none -> 37 us  [per_device(): lax.all_to_all(jnp.broadcast_to(eight[None], (32, 8, half)), CHIPS, 0, 0,...]
    all_to_all x0 -> x1, waiting for transfers between devices: none -> 29 us  [per_device(): pieces = lax.all_to_all(total.reshape(32, 8, half), CHIPS, 0, 0, tiled=True)]
    ppermute x0 -> x5, waiting for transfers between devices: none -> 13.2 us  [the longest x4 10.5 us: swap_core(): return lax.ppermute(v, ALL, pairs)]
    dot_general x2 -> x3, matrix products: 17.1 us -> 4.27 us  [the longest x2 2.83 us: rows_of(): lax.dot_general(left, weight, (((1,), (1,)), ((), ())), preferred_element...]
    unnamed x1 -> x6, local copies, waits for them, and re-layouts: 6.92 us -> 0.74 us
    all_to_all x0 -> x1, starting transfers between devices: none -> 5.02 us  [per_device(): pieces = lax.all_to_all(total.reshape(32, 8, half), CHIPS, 0, 0, tiled=True)]
  transfers between devices with their start and end apart: 1 -> 6, of which waited for: 1 -> 6; matrix products, arithmetic and copies ran while one was open for 0% -> 0% of each run, Pallas kernels for 0% -> 0%
where the time goes in v1:
time: 99 us; the launch traced here: 97.7 us
  waiting for transfers between devices  42.2 us (43%)
  blocking collectives  37 us (37%)
  starting transfers between devices  8.23 us (8%)
  other arithmetic  4.75 us (5%)
  matrix products  4.27 us (4%)
  local copies, waits for them, and re-layouts  1.05 us (1%)
    all_to_all x1, blocking collectives, per_device(): lax.all_to_all(jnp.broadcast_to(eight[None], (32, 8, half)), CHIPS, 0, 0,...  37 us
    all_to_all x1, waiting for transfers between devices, per_device(): pieces = lax.all_to_all(total.reshape(32, 8, half), CHIPS, 0, 0, tiled=True)  29 us
    ppermute x4, waiting for transfers between devices, swap_core(): return lax.ppermute(v, ALL, pairs)  10.5 us
    all_to_all x1, starting transfers between devices, per_device(): pieces = lax.all_to_all(total.reshape(32, 8, half), CHIPS, 0, 0, tiled=True)  5.02 us
    dot_general x2, matrix products, rows_of(): lax.dot_general(left, weight, (((1,), (1,)), ((), ())), preferred_element...  2.83 us
    ppermute x1, starting transfers between devices, swap_far(): return lax.ppermute(v, ALL, pairs)  2.81 us
    ppermute x1, waiting for transfers between devices, swap_far(): return lax.ppermute(v, ALL, pairs)  2.68 us
    reshape x1, other arithmetic, per_device(): pieces = lax.all_to_all(total.reshape(32, 8, half), CHIPS, 0, 0, tiled=True)  2.3 us
  transfers between devices with their start and end apart: 6, of which 6 were waited for; matrix products, arithmetic and copies ran while one was open for 0% of the time, Pallas kernels for 0%

profile of v1, /device:TPU:0, one launch (start us, length us, event | category | flops | bytes accessed | tf_op | source)
XLA Modules:
  0.0 97.7 jit_solution(6609297284486682853)
XLA Ops:
  0.0 0.0 copy-start.1
  0.0 1.0 broadcast_select_fusion.2
  1.0 0.1 collective-permute-start
  1.1 1.2 %collective-permute-done = bf16[4,4096]{1,0:T(4,128)(2,1)S(1)} collective-permute-done((bf16[4,4096]{1,0:T(4,128)(2,1)S(1)}, bf16[4,4096]{1,0:T(4,128)(2,1)S(1)}, u32[]{:S(2)}, u32[]{:S(2)}) %collective-permute-start) | collective-permute-done | bytes 32800 | tf_op jit(solution)/shard_map/pre/ppermute | solution.py:27
  2.3 0.1 maximum_select_fusion.3
  2.3 0.2 broadcast_in_dim.2
  2.6 37.0 %all_to_all.10 = bf16[32,8,4096]{2,1,0:T(8,128)(2,1)S(1)} all-to-all(bf16[32,8,4096]{2,1,0:T(8,128)(2,1)S(1)} %broadcast_in_dim.2), channel_id=1, replica_groups=mesh['xl'=2,'y'=4,'z'=4,'c'=2,'xh'=2] {'xl','y','z'}, dimensions={0} | all-to-all | bytes 4194304 | tf_op jit(solution)/shard_map/gather/all_to_all | solution.py:53
  39.6 0.0 copy-start.2
  39.6 0.0 collective-permute-start.1
  39.6 4.2 %collective-permute-done.1 = bf16[256,4096]{1,0:T(8,128)(2,1)S(1)} collective-permute-done((bf16[256,4096]{1,0:T(8,128)(2,1)S(1)}, bf16[256,4096]{1,0:T(8,128)(2,1)S(1)}, u32[]{:S(2)}, u32[]{:S(2)}) %collective-permute-start.1) | collective-permute-done | bytes 2097184 | tf_op jit(solution)/shard_map/share/ppermute | solution.py:27
  43.7 0.0 copy-done.1
  43.7 1.5 %fusion.1 = f32[256,231]{0,1:T(8,128)S(1)} fusion(bf16[231,8192]{1,0:T(8,128)(2,1)S(1)} %copy-done.1, bf16[256,4096]{1,0:T(8,128)(2,1)S(1)} %collective-permute-done.1, bf16[256,4096]{1,0:T(8,128)(2,1)S(1)} %bitcast.37, pred[]{:T(512)S(6)} %eq.4), kind=kOutput, calls=%fused_computation.5 | convolution fusion | flops 987758592 | bytes 8215553 | tf_op jit(solution)/shard_map/dot_general | solution.py:36
  45.3 0.0 copy-done.2
  45.3 0.0 copy-start
  45.3 1.3 %fusion.2 = f32[256,231]{0,1:T(8,128)S(1)} fusion(bf16[231,8192]{1,0:T(8,128)(2,1)S(1)} %copy-done.2, bf16[256,4096]{1,0:T(8,128)(2,1)S(1)} %collective-permute-done.1, bf16[256,4096]{1,0:T(8,128)(2,1)S(1)} %bitcast.38, pred[]{:T(512)S(6)} %eq.4), kind=kOutput, calls=%fused_computation.6 | convolution fusion | flops 987758592 | bytes 8215553 | tf_op jit(solution)/shard_map/dot_general | solution.py:36
  46.6 0.7 copy-done
  47.3 1.4 %fusion.3 = f32[256,8192]{1,0:T(8,128)S(1)} fusion(bf16[231,8192]{1,0:T(8,128)(2,1)S(1)} %copy-done, f32[256,231]{0,1:T(8,128)S(1)} %fusion.1, f32[256,231]{0,1:T(8,128)S(1)} %fusion.2), kind=kOutput, calls=%fused_computation.9 | convolution fusion | flops 969239040 | bytes 12646400 | tf_op jit(solution)/shard_map/dot_general | solution.py:66
  48.8 0.4 select_convert_fusion
  49.2 0.2 collective-permute-start.2
  49.4 4.0 %collective-permute-done.2 = bf16[256,4096]{1,0:T(8,128)(2,1)S(1)} collective-permute-done((bf16[256,4096]{1,0:T(8,128)(2,1)S(1)}, bf16[256,4096]{1,0:T(8,128)(2,1)S(1)}, u32[]{:S(2)}, u32[]{:S(2)}) %collective-permute-start.2) | collective-permute-done | bytes 2097184 | tf_op jit(solution)/shard_map/fold/ppermute | solution.py:27
  53.4 2.3 %fusion = bf16[32,8,4096]{2,1,0:T(8,128)(2,1)} fusion(bf16[256,4096]{1,0:T(8,128)(2,1)S(1)} %collective-permute-done.2, f32[256,8192]{1,0:T(8,128)S(1)} %fusion.3, pred[]{:T(512)S(6)} %eq.4), kind=kLoop, calls=%fused_computation.4 | loop fusion | flops 4194304 | bytes 12582913 | tf_op jit(solution)/shard_map/scatter/reshape | solution.py:73
  55.7 5.0 %all-to-all-start.1 = ((bf16[32,8,4096]{2,1,0:T(8,128)(2,1)}), bf16[32,8,4096]{2,1,0:T(8,128)(2,1)S(1)}, u32[]{:S(2)}, u32[]{:S(2)}) async-start(bf16[32,8,4096]{2,1,0:T(8,128)(2,1)} %fusion), calls=%async_computation.1 | async-start | bytes 4194304 | tf_op jit(solution)/shard_map/scatter/all_to_all | solution.py:73
  60.7 29.0 %all-to-all-done.1 = bf16[32,8,4096]{2,1,0:T(8,128)(2,1)S(1)} async-done(((bf16[32,8,4096]{2,1,0:T(8,128)(2,1)}), bf16[32,8,4096]{2,1,0:T(8,128)(2,1)S(1)}, u32[]{:S(2)}, u32[]{:S(2)}) %all-to-all-start.1) | async-done | bytes 2097184 | tf_op jit(solution)/shard_map/scatter/all_to_all | solution.py:73
  89.8 0.3 convert_reduce_fusion
  90.0 0.1 reshape.49
  90.2 2.8 %collective-permute-start.3 = (bf16[2,2,4096]{2,1,0:T(2,128)(2,1)S(1)}, bf16[2,2,4096]{2,1,0:T(2,128)(2,1)S(1)}, u32[]{:S(2)}, u32[]{:S(2)}) collective-permute-start(bf16[2,2,4096]{2,1,0:T(2,128)(2,1)S(1)} %fusion.9), channel_id=1, source_target_pairs={{0,1},{1,0},{2,3},{3,2},{4,5},{5,4},{6,7},{7,6},{8,9},{9,8},{10,11... | collective-permute-start | bytes 98312 | tf_op jit(solution)/shard_map/far/ppermute | solution.py:32
  93.0 2.7 %collective-permute-done.3 = bf16[2,2,4096]{2,1,0:T(2,128)(2,1)S(1)} collective-permute-done((bf16[2,2,4096]{2,1,0:T(2,128)(2,1)S(1)}, bf16[2,2,4096]{2,1,0:T(2,128)(2,1)S(1)}, u32[]{:S(2)}, u32[]{:S(2)}) %collective-permute-start.3) | collective-permute-done | bytes 32800 | tf_op jit(solution)/shard_map/far/ppermute | solution.py:32
  95.7 0.1 fusion.8
  95.8 0.1 collective-permute-start.4
  95.9 1.2 %collective-permute-done.4 = bf16[2,4096]{1,0:T(2,128)(2,1)S(1)} collective-permute-done((bf16[2,4096]{1,0:T(2,128)(2,1)S(1)}, bf16[2,4096]{1,0:T(2,128)(2,1)S(1)}, u32[]{:S(2)}, u32[]{:S(2)}) %collective-permute-start.4) | collective-permute-done | bytes 16416 | tf_op jit(solution)/shard_map/post/ppermute | solution.py:27
  97.0 0.7 broadcast_select_fusion
  (2 shorter events, 0.1 us)
Async XLA Ops:
  0.0 43.7 %copy-start.1 = (bf16[231,8192]{1,0:T(8,128)(2,1)S(1)}, bf16[231,8192]{1,0:T(8,128)(2,1)}, u32[]{:S(2)}) copy-start(bf16[231,8192]{1,0:T(8,128)(2,1)} %param.6) | copy-start | bytes 11354116
  1.0 1.3 %collective-permute-start = (bf16[4,4096]{1,0:T(4,128)(2,1)S(1)}, bf16[4,4096]{1,0:T(4,128)(2,1)S(1)}, u32[]{:S(2)}, u32[]{:S(2)}) collective-permute-start(bf16[4,4096]{1,0:T(4,128)(2,1)S(1)} %get-tuple-element.6), channel_id=1, source_target_pairs={{0,2},{1,3},{2,0},{3,1},{4,6},{5,7},{6,4},{7,5},{8,10},{9,11},{10,... | collective-permute-start | bytes 98312 | tf_op jit(solution)/shard_map/pre/ppermute | solution.py:27
  39.6 5.7 %copy-start.2 = (bf16[231,8192]{1,0:T(8,128)(2,1)S(1)}, bf16[231,8192]{1,0:T(8,128)(2,1)}, u32[]{:S(2)}) copy-start(bf16[231,8192]{1,0:T(8,128)(2,1)} %param.5) | copy-start | bytes 11354116
  39.6 4.2 %collective-permute-start.1 = (bf16[256,4096]{1,0:T(8,128)(2,1)S(1)}, bf16[256,4096]{1,0:T(8,128)(2,1)S(1)}, u32[]{:S(2)}, u32[]{:S(2)}) collective-permute-start(bf16[256,4096]{1,0:T(8,128)(2,1)S(1)} %bitcast.36), channel_id=1, source_target_pairs={{0,2},{1,3},{2,0},{3,1},{4,6},{5,7},{6,4},{7,5},{8,10},{9,11},{10,... | collective-permute-start | bytes 6291464 | tf_op jit(solution)/shard_map/share/ppermute | solution.py:27
  45.3 2.1 %copy-start = (bf16[231,8192]{1,0:T(8,128)(2,1)S(1)}, bf16[231,8192]{1,0:T(8,128)(2,1)}, u32[]{:S(2)}) copy-start(bf16[231,8192]{1,0:T(8,128)(2,1)} %param.7) | copy-start | bytes 11354116
  49.2 4.2 %collective-permute-start.2 = (bf16[256,4096]{1,0:T(8,128)(2,1)S(1)}, bf16[256,4096]{1,0:T(8,128)(2,1)S(1)}, u32[]{:S(2)}, u32[]{:S(2)}) collective-permute-start(bf16[256,4096]{1,0:T(8,128)(2,1)S(1)} %select_convert_fusion), channel_id=1, source_target_pairs={{0,2},{1,3},{2,0},{3,1},{4,6},{5,7},{6,4},{7,5},{8,10},{9,11},{10,... | collective-permute-start | bytes 6291464 | tf_op jit(solution)/shard_map/fold/ppermute | solution.py:27
  55.7 34.1 %all-to-all-start.1 = ((bf16[32,8,4096]{2,1,0:T(8,128)(2,1)}), bf16[32,8,4096]{2,1,0:T(8,128)(2,1)S(1)}, u32[]{:S(2)}, u32[]{:S(2)}) async-start(bf16[32,8,4096]{2,1,0:T(8,128)(2,1)} %fusion), calls=%async_computation.1 | async-start | bytes 4194304 | tf_op jit(solution)/shard_map/scatter/all_to_all | solution.py:73
  90.2 5.5 %collective-permute-start.3 = (bf16[2,2,4096]{2,1,0:T(2,128)(2,1)S(1)}, bf16[2,2,4096]{2,1,0:T(2,128)(2,1)S(1)}, u32[]{:S(2)}, u32[]{:S(2)}) collective-permute-start(bf16[2,2,4096]{2,1,0:T(2,128)(2,1)S(1)} %fusion.9), channel_id=1, source_target_pairs={{0,1},{1,0},{2,3},{3,2},{4,5},{5,4},{6,7},{7,6},{8,9},{9,8},{10,11... | collective-permute-start | bytes 98312 | tf_op jit(solution)/shard_map/far/ppermute | solution.py:32
  95.8 1.3 %collective-permute-start.4 = (bf16[2,4096]{1,0:T(2,128)(2,1)S(1)}, bf16[2,4096]{1,0:T(2,128)(2,1)S(1)}, u32[]{:S(2)}, u32[]{:S(2)}) collective-permute-start(bf16[2,4096]{1,0:T(2,128)(2,1)S(1)} %get-tuple-element.8), channel_id=1, source_target_pairs={{0,2},{1,3},{2,0},{3,1},{4,6},{5,7},{6,4},{7,5},{8,10},{9,11},{10,... | collective-permute-start | bytes 49160 | tf_op jit(solution)/shard_map/post/ppermute | solution.py:27

commit v2 on v1

v2 whole, which is shorter than its diff:
```python
import jax
import jax.numpy as jnp
from jax import lax
from jax.experimental import pallas as pl
from jax.experimental.pallas import tpu as pltpu
from jax.sharding import Mesh, PartitionSpec as P

ALL = ("xl", "y", "z", "c", "xh")
PLANE = ("xl", "y", "z")
CHIPS = ("xl", "y", "z", "xh")
BF = jnp.bfloat16
F32 = jnp.float32


def flat(xl, y, z, c, xh):
    return (((xl * 4 + y) * 4 + z) * 2 + c) * 2 + xh


def every():
    for xl in range(2):
        for y in range(4):
            for z in range(4):
                for c in range(2):
                    for xh in range(2):
                        yield xl, y, z, c, xh


def swap_core(v):
    pairs = [(flat(a, y, z, c, h), flat(a, y, z, 1 - c, h)) for a, y, z, c, h in every()]
    return lax.ppermute(v, ALL, pairs)


def rows_of(left, weight):
    return lax.dot_general(
        left, weight, (((1,), (1,)), ((), ())), preferred_element_type=F32
    )


def hidden_kernel(x_ref, gate_ref, up_ref, hidden_ref):
    x = x_ref[...].reshape(128, x_ref.shape[2])
    gate = rows_of(x, gate_ref[...])
    up = rows_of(x, up_ref[...])
    hidden_ref[...] = (gate / (1.0 + jnp.exp(-gate)) * up).astype(BF)


def down_kernel(hidden_ref, down_ref, out_ref):
    part = jnp.dot(hidden_ref[...], down_ref[...], preferred_element_type=F32)
    out_ref[...] = part.astype(BF).reshape(out_ref.shape)


def fold_kernel(hidden_ref, down_ref, other_ref, out_ref):
    part = jnp.dot(hidden_ref[...], down_ref[...], preferred_element_type=F32)
    other = other_ref[...].reshape(part.shape).astype(F32)
    out_ref[...] = (part + other).astype(BF).reshape(out_ref.shape)


VM = pl.BlockSpec(memory_space=pltpu.VMEM)


def call(kernel, shape, *args):
    return pl.pallas_call(
        kernel,
        out_shape=jax.ShapeDtypeStruct(shape, BF),
        in_specs=[VM] * len(args),
        out_specs=VM,
        compiler_params=pltpu.CompilerParams(vmem_limit_bytes=24 * 2**20),
    )(*args)


def per_device(tokens, gate_weight, up_weight, down_weight):
    rows, d = tokens.shape
    f = gate_weight.shape[0]
    with jax.named_scope("pre"):
        block = swap_core(tokens)
    with jax.named_scope("gather"):
        near = lax.all_to_all(
            jnp.broadcast_to(block[None], (32, rows, d)), PLANE, 0, 0, tiled=True
        )
    with jax.named_scope("share"):
        far = swap_core(near)
    with jax.named_scope("near"):
        hidden = call(hidden_kernel, (128, f), near, gate_weight, up_weight)
        part = call(down_kernel, (64, 2, d), hidden, down_weight)
    with jax.named_scope("fold"):
        part = swap_core(part)
    with jax.named_scope("far"):
        hidden = call(hidden_kernel, (128, f), far, gate_weight, up_weight)
        part = call(fold_kernel, (64, 2, d), hidden, down_weight, part)
    with jax.named_scope("scatter"):
        pieces = lax.all_to_all(part, CHIPS, 0, 0, tiled=True)
    return jnp.sum(pieces.astype(F32), axis=0).astype(BF)


def solution(mesh):
    fine = Mesh(mesh.devices.reshape(2, 4, 4, 2, 2), ALL)
    return jax.shard_map(
        per_device,
        mesh=fine,
        in_specs=(P(("xl", "y", "z", "c"), None), P(ALL, None), P(ALL, None), P(ALL, None)),
        out_specs=P(ALL, None),
        check_vma=False,
    )
```

time: 99 us -> 91.2 us (0.921); the launches traced: 97.7 us -> 91 us
  waiting for transfers between devices: 42.2 us -> 1.86 us
  blocking collectives: 37 us -> 74.4 us
  Pallas kernels: 0 us -> 7.83 us
  starting transfers between devices: 8.23 us -> 0.6 us
  matrix products: 4.27 us -> 0 us
  local copies, waits for them, and re-layouts: 1.05 us -> 3.66 us
  other arithmetic: 4.75 us -> 2.54 us
    all_to_all x1 -> x2, blocking collectives: 37 us -> 74.4 us  [the longest x1 37.3 us: per_device(): lax.all_to_all(jnp.broadcast_to(block[None], (32, rows, d)), PLANE, 0, 0,...]
    all_to_all x1 -> x0, waiting for transfers between devices: 29 us -> none  [per_device(): pieces = lax.all_to_all(total.reshape(32, 8, half), CHIPS, 0, 0, tiled=True)]
    ppermute x4 -> x3, waiting for transfers between devices: 10.5 us -> 1.86 us  [swap_core(): return lax.ppermute(v, ALL, pairs)]
    pallas_call x0 -> x4, Pallas kernels: none -> 7.83 us  [call(): pl.pallas_call(kernel, out_shape=jax.ShapeDtypeStruct(shape, BF), in_spec...]
    all_to_all x1 -> x0, starting transfers between devices: 5.02 us -> none  [per_device(): pieces = lax.all_to_all(total.reshape(32, 8, half), CHIPS, 0, 0, tiled=True)]
    dot_general x3 -> x0, matrix products: 4.27 us -> none  [the longest x2 2.83 us: rows_of(): lax.dot_general(left, weight, (((1,), (1,)), ((), ())), preferred_element...]
    ppermute x1 -> x0, starting transfers between devices: 2.81 us -> none  [swap_far(): return lax.ppermute(v, ALL, pairs)]
    ppermute x1 -> x0, waiting for transfers between devices: 2.68 us -> none  [swap_far(): return lax.ppermute(v, ALL, pairs)]
  transfers between devices with their start and end apart: 6 -> 3, of which waited for: 6 -> 2; matrix products, arithmetic and copies ran while one was open for 0% -> 0% of each run, Pallas kernels for 0% -> 7%
where the time goes in v2:
time: 91.2 us; the launch traced here: 91 us
  blocking collectives  74.4 us (82%)
  Pallas kernels  7.83 us (9%)
  local copies, waits for them, and re-layouts  3.66 us (4%)
  other arithmetic  2.54 us (3%)
  waiting for transfers between devices  1.86 us (2%)
    all_to_all x1, blocking collectives, per_device(): lax.all_to_all(jnp.broadcast_to(block[None], (32, rows, d)), PLANE, 0, 0,...  37.3 us
    all_to_all x1, blocking collectives, per_device(): pieces = lax.all_to_all(part, CHIPS, 0, 0, tiled=True)  37.2 us
    pallas_call x4, Pallas kernels, call(): pl.pallas_call(kernel, out_shape=jax.ShapeDtypeStruct(shape, BF), in_spec...  7.83 us
    unnamed x8, local copies, waits for them, and re-layouts  2.73 us
    reduce_sum x1, other arithmetic, per_device(): return jnp.sum(pieces.astype(F32), axis=0).astype(BF)  2.54 us
    ppermute x3, waiting for transfers between devices, swap_core(): return lax.ppermute(v, ALL, pairs)  1.86 us
  transfers between devices with their start and end apart: 3, of which 2 were waited for; matrix products, arithmetic and copies ran while one was open for 0% of the time, Pallas kernels for 7%

profile of v2, /device:TPU:0, one launch (start us, length us, event | category | flops | bytes accessed | tf_op | source)
XLA Modules:
  0.0 91.0 jit_solution(3119048126362879338)
XLA Ops:
  0.0 0.0 collective-permute-start
  0.0 1.5 %collective-permute-done = bf16[4,8192]{1,0:T(4,128)(2,1)S(1)} collective-permute-done((bf16[4,8192]{1,0:T(4,128)(2,1)}, bf16[4,8192]{1,0:T(4,128)(2,1)S(1)}, u32[]{:S(2)}, u32[]{:S(2)}) %collective-permute-start) | collective-permute-done | bytes 65568 | tf_op jit(solution)/shard_map/pre/ppermute | solution.py:30
  1.5 0.9 %broadcast_in_dim.2 = bf16[32,4,8192]{2,1,0:T(4,128)(2,1)S(1)} broadcast(bf16[4,8192]{1,0:T(4,128)(2,1)S(1)} %collective-permute-done), dimensions={1,2} | broadcast | bytes 2162688 | tf_op jit(solution)/shard_map/gather/broadcast_in_dim | solution.py:77
  2.4 0.0 copy-start
  2.4 37.3 %all_to_all.10.x_ref = bf16[32,4,8192]{2,1,0:T(4,128)(2,1)S(1)} all-to-all(bf16[32,4,8192]{2,1,0:T(4,128)(2,1)S(1)} %broadcast_in_dim.2), channel_id=1, replica_groups=mesh['xl'=2,'y'=4,'z'=4,'c'=2,'xh'=2] {'xl','y','z'}, dimensions={0} | all-to-all | bytes 4194304 | tf_op jit(solution)/shard_map/gather/all_to_all | solution.py:76
  39.7 0.0 collective-permute-start.1
  39.7 0.0 copy-done
  39.7 0.0 copy-start.1
  39.7 2.1 %copy-done.1 = bf16[231,8192]{1,0:T(8,128)(2,1)S(1)} copy-done((bf16[231,8192]{1,0:T(8,128)(2,1)S(1)}, bf16[231,8192]{1,0:T(8,128)(2,1)}, u32[]{:S(2)}) %copy-start.1) | copy-done | bytes 3784728
  41.8 0.0 copy-start.3
  41.8 2.7 %near.2.hidden_ref = bf16[128,231]{1,0:T(8,128)(2,1)S(1)} custom-call(bf16[32,4,8192]{2,1,0:T(4,128)(2,1)S(1)} %all_to_all.10.x_ref, bf16[231,8192]{1,0:T(8,128)(2,1)S(1)} %copy-done, bf16[231,8192]{1,0:T(8,128)(2,1)S(1)} %copy-done.1), custom_call_target="tpu_custom_call" | custom-call | tf_op jit(solution)/shard_map/near/pallas_call | solution.py:61
  44.5 0.0 copy-done.3
  44.6 0.0 copy-start.2
  44.6 0.8 near.3
  45.4 0.6 collective-permute-start.2
  46.0 0.0 collective-permute-done.1.x_ref
  46.0 0.6 copy-done.2
  46.6 2.7 %far.2.hidden_ref = bf16[128,231]{1,0:T(8,128)(2,1)S(1)} custom-call(bf16[32,4,8192]{2,1,0:T(4,128)(2,1)S(1)} %collective-permute-done.1.x_ref, bf16[231,8192]{1,0:T(8,128)(2,1)S(1)} %copy-done, bf16[231,8192]{1,0:T(8,128)(2,1)S(1)} %copy-done.2), custom_call_target="tpu_custom_call" | custom-call | tf_op jit(solution)/shard_map/far/pallas_call | solution.py:61
  49.4 0.4 collective-permute-done.2.other_ref
  49.8 1.5 %far.3 = bf16[64,2,8192]{2,1,0:T(2,128)(2,1)S(1)} custom-call(bf16[128,231]{1,0:T(8,128)(2,1)S(1)} %far.2.hidden_ref, bf16[231,8192]{1,0:T(8,128)(2,1)S(1)} %copy-done.3, bf16[64,2,8192]{2,1,0:T(2,128)(2,1)S(1)} %collective-permute-done.2.other_ref), custom_call_target="tpu_custom_call" | custom-call | tf_op jit(solution)/shard_map/far/pallas_call | solution.py:61
  51.3 37.2 %all_to_all.11 = bf16[64,2,8192]{2,1,0:T(2,128)(2,1)S(1)} all-to-all(bf16[64,2,8192]{2,1,0:T(2,128)(2,1)S(1)} %far.3), channel_id=1, replica_groups=mesh['xl'=2,'y'=4,'z'=4,'c'=2,'xh'=2] {'xl','y','z','xh'}, dimensions={0} | all-to-all | bytes 4194304 | tf_op jit(solution)/shard_map/scatter/all_to_all | solution.py:90
  88.5 2.5 %reduce_sum.12 = bf16[2,8192]{1,0:T(2,128)(2,1)} reduce(bf16[64,2,8192]{2,1,0:T(2,128)(2,1)S(1)} %all_to_all.11, bf16[]{:T(256)} %constant.2.clone.1), dimensions={0}, to_apply=%region_0.0 | reduce | flops 1032192 | bytes 2129922 | tf_op jit(solution)/shard_map/reduce_sum | solution.py:91
Async XLA Ops:
  0.0 1.5 %collective-permute-start = (bf16[4,8192]{1,0:T(4,128)(2,1)}, bf16[4,8192]{1,0:T(4,128)(2,1)S(1)}, u32[]{:S(2)}, u32[]{:S(2)}) collective-permute-start(bf16[4,8192]{1,0:T(4,128)(2,1)} %param.4), channel_id=1, source_target_pairs={{0,2},{1,3},{2,0},{3,1},{4,6},{5,7},{6,4},{7,5},{8,10},{9,11},{10,... | collective-permute-start | bytes 196616 | tf_op jit(solution)/shard_map/pre/ppermute | solution.py:30
  2.4 37.3 %copy-start = (bf16[231,8192]{1,0:T(8,128)(2,1)S(1)}, bf16[231,8192]{1,0:T(8,128)(2,1)}, u32[]{:S(2)}) copy-start(bf16[231,8192]{1,0:T(8,128)(2,1)} %gate_ref.3) | copy-start | bytes 11354116
  39.7 6.3 %collective-permute-start.1 = (bf16[32,4,8192]{2,1,0:T(4,128)(2,1)S(1)}, bf16[32,4,8192]{2,1,0:T(4,128)(2,1)S(1)}, u32[]{:S(2)}, u32[]{:S(2)}) collective-permute-start(bf16[32,4,8192]{2,1,0:T(4,128)(2,1)S(1)} %all_to_all.10.x_ref), channel_id=1, source_target_pairs={{0,2},{1,3},{2,0},{3,1},{4,6},{5,7},{6,4},{7,5},{8,10},{9,11},{10,... | collective-permute-start | bytes 6291464 | tf_op jit(solution)/shard_map/share/ppermute | solution.py:30
  39.7 2.1 %copy-start.1 = (bf16[231,8192]{1,0:T(8,128)(2,1)S(1)}, bf16[231,8192]{1,0:T(8,128)(2,1)}, u32[]{:S(2)}) copy-start(bf16[231,8192]{1,0:T(8,128)(2,1)} %up_ref.3) | copy-start | bytes 11354116
  41.8 2.8 %copy-start.3 = (bf16[231,8192]{1,0:T(8,128)(2,1)S(1)}, bf16[231,8192]{1,0:T(8,128)(2,1)}, u32[]{:S(2)}) copy-start(bf16[231,8192]{1,0:T(8,128)(2,1)} %down_ref.3) | copy-start | bytes 11354116
  44.6 2.1 %copy-start.2 = (bf16[231,8192]{1,0:T(8,128)(2,1)S(1)}, bf16[231,8192]{1,0:T(8,128)(2,1)}, u32[]{:S(2)}) copy-start(bf16[231,8192]{1,0:T(8,128)(2,1)} %up_ref.3) | copy-start | bytes 11354116
  45.4 4.4 %collective-permute-start.2 = (bf16[64,2,8192]{2,1,0:T(2,128)(2,1)S(1)}, bf16[64,2,8192]{2,1,0:T(2,128)(2,1)S(1)}, u32[]{:S(2)}, u32[]{:S(2)}) collective-permute-start(bf16[64,2,8192]{2,1,0:T(2,128)(2,1)S(1)} %near.3), channel_id=1, source_target_pairs={{0,2},{1,3},{2,0},{3,1},{4,6},{5,7},{6,4},{7,5},{8,10},{9,11},{10,... | collective-permute-start | bytes 6291464 | tf_op jit(solution)/shard_map/fold/ppermute | solution.py:30

commit v3 on v2

v3 whole, which is shorter than its diff:
```python
import jax
import jax.numpy as jnp
from jax import lax
from jax.experimental import pallas as pl
from jax.experimental.pallas import tpu as pltpu
from jax.sharding import Mesh, PartitionSpec as P


ALL = ("xl", "y", "z", "c", "xh")
BF = jnp.bfloat16
F32 = jnp.float32


def move(v, to):
    def flat(x, y, z, c):
        return (((x % 2 * 4 + y) * 4 + z) * 2 + c) * 2 + x // 2

    pairs = []
    for x in range(4):
        for y in range(4):
            for z in range(4):
                for c in range(2):
                    tx, tc = to(x, c)
                    pairs.append((flat(x, y, z, c), flat(tx, y, z, tc)))
    return lax.ppermute(v, ALL, pairs)


def core(v):
    return move(v, lambda x, c: (x, 1 - c))


def inner(v):
    return move(v, lambda x, c: (x ^ 1, c))


def outer(v):
    return move(v, lambda x, c: (3 - x, c))


def rows_of(left, weight):
    return lax.dot_general(
        left, weight, (((1,), (1,)), ((), ())), preferred_element_type=F32
    )


def hidden_kernel(*refs):
    *x_refs, gate_ref, up_ref, hidden_ref = refs
    d = x_refs[0].shape[2]
    x = jnp.concatenate([r[...].reshape(-1, d) for r in x_refs], axis=0)
    gate = rows_of(x, gate_ref[...])
    up = rows_of(x, up_ref[...])
    hidden_ref[...] = (gate / (1.0 + jnp.exp(-gate)) * up).astype(BF)


def down_kernel(at, n_out, *refs):
    hidden_ref, down_ref, *more = refs[:-n_out]
    outs = refs[-n_out:]
    rows = sum(o.shape[0] for o in outs) * 2
    part = jnp.dot(
        hidden_ref[at : at + rows, :], down_ref[...], preferred_element_type=F32
    )
    if more:
        part += more[0][...].reshape(part.shape).astype(F32)
    if more[1:]:
        part += jnp.concatenate(
            [r[...].reshape(rows // 2, -1) for r in more[1:]], axis=0
        ).astype(F32)
    each = rows // n_out
    for i, o in enumerate(outs):
        o[...] = part[i * each : (i + 1) * each].astype(BF).reshape(o.shape)


VM = pl.BlockSpec(memory_space=pltpu.VMEM)


def call(kernel, shapes, *args):
    return pl.pallas_call(
        kernel,
        out_shape=[jax.ShapeDtypeStruct(shape, BF) for shape in shapes],
        in_specs=[VM] * len(args),
        out_specs=[VM] * len(shapes),
        compiler_params=pltpu.CompilerParams(vmem_limit_bytes=20 * 2**20),
    )(*args)


def down(at, shapes, *args):
    return call(lambda *refs: down_kernel(at, len(shapes), *refs), shapes, *args)


def per_device(tokens, *weights):
    rows, d = tokens.shape
    f = weights[0].shape[0]
    block = inner(tokens)
    gate_weight, up_weight, down_weight = weights
    away = lax.all_to_all(
        jnp.broadcast_to(block[None], (16, rows, d)), ("y", "z"), 0, 0, tiled=True
    )
    away_sib = core(away)
    home_a = inner(away[:8])
    home_b = outer(away[8:])
    (hidden,) = call(hidden_kernel, [(128, f)], away, away_sib, gate_weight, up_weight)
    (part,) = down(64, [(32, 2, d)], hidden, down_weight)
    part = core(part)
    part_a, part_b = down(0, [(16, 2, d)] * 2, hidden, down_weight, part)
    back_a = inner(part_a)
    back_b = outer(part_b)
    sib_a = core(home_a)
    sib_b = core(home_b)
    (hidden,) = call(
        hidden_kernel,
        [(128, f)],
        home_a,
        home_b,
        sib_a,
        sib_b,
        gate_weight,
        up_weight,
    )
    (part,) = down(64, [(32, 2, d)], hidden, down_weight)
    part = core(part)
    (part,) = down(
        0, [(32, 2, d)], hidden, down_weight, part, back_a, back_b
    )
    pieces = lax.all_to_all(part, ("y", "z", "xh"), 0, 0, tiled=True)
    return jnp.sum(pieces.astype(F32), axis=0).astype(BF)


def solution(mesh):
    fine = Mesh(mesh.devices.reshape(2, 4, 4, 2, 2), ALL)

    return jax.shard_map(
        per_device,
        mesh=fine,
        in_specs=(P(("xl", "y", "z", "c"), None), P(ALL, None), P(ALL, None), P(ALL, None)),
        out_specs=P(ALL, None),
        check_vma=False,
    )
```

time: 91.2 us -> 100 us (1.096)
  waiting for transfers between devices: 1.86 us -> 30.3 us
  blocking collectives: 74.4 us -> 47.6 us
  starting transfers between devices: 0.6 us -> 7.52 us
  Pallas kernels: 7.83 us -> 9.43 us
    ppermute x3 -> x10, waiting for transfers between devices: 1.86 us -> 30.3 us  [move(): return lax.ppermute(v, ALL, pairs)]
    all_to_all x2, blocking collectives: 74.4 us -> 47.6 us  [the longest x1 23.9 us: per_device(): lax.all_to_all(jnp.broadcast_to(block[None], (16, rows, d)), ('y', 'z'),...]
    ppermute x3 -> x10, starting transfers between devices: 0.6 us -> 7.52 us  [move(): return lax.ppermute(v, ALL, pairs)]
    pallas_call x4 -> x6, Pallas kernels: 7.83 us -> 9.43 us  [call(): pl.pallas_call(kernel, out_shape=[jax.ShapeDtypeStruct(shape, BF) for sha...]
  transfers between devices with their start and end apart: 3 -> 10, of which waited for: 2 -> 5; matrix products, arithmetic and copies ran while one was open for 0% -> 0% of each run, Pallas kernels for 7% -> 8%
where the time goes in v3:
time: 100 us
  blocking collectives  47.6 us (48%)
  waiting for transfers between devices  30.3 us (30%)
  Pallas kernels  9.43 us (9%)
  starting transfers between devices  7.52 us (8%)
  local copies, waits for them, and re-layouts  3.5 us (4%)
  other arithmetic  1.58 us (2%)
    ppermute x10, waiting for transfers between devices, move(): return lax.ppermute(v, ALL, pairs)  30.3 us
    all_to_all x1, blocking collectives, per_device(): lax.all_to_all(jnp.broadcast_to(block[None], (16, rows, d)), ('y', 'z'),...  23.9 us
    all_to_all x1, blocking collectives, per_device(): pieces = lax.all_to_all(part, ('y', 'z', 'xh'), 0, 0, tiled=True)  23.7 us
    pallas_call x6, Pallas kernels, call(): pl.pallas_call(kernel, out_shape=[jax.ShapeDtypeStruct(shape, BF) for sha...  9.43 us
    ppermute x10, starting transfers between devices, move(): return lax.ppermute(v, ALL, pairs)  7.52 us
    unnamed x8, local copies, waits for them, and re-layouts  2.71 us
  transfers between devices with their start and end apart: 10, of which 5 were waited for; matrix products, arithmetic and copies ran while one was open for 0% of the time, Pallas kernels for 8%

profile of v3, /device:TPU:0, one launch (start us, length us, event | category | flops | bytes accessed | tf_op | source)
XLA Modules:
  0.0 100.0 jit_solution(21760890761465596)
XLA Ops:
  0.0 1.6 %collective-permute-start = (bf16[4,8192]{1,0:T(4,128)(2,1)}, bf16[4,8192]{1,0:T(4,128)(2,1)S(1)}, u32[]{:S(2)}, u32[]{:S(2)}) collective-permute-start(bf16[4,8192]{1,0:T(4,128)(2,1)} %param.4), channel_id=1, source_target_pairs={{0,64},{2,66},{4,68},{6,70},{8,72},{10,74},{12,76},{14,78},{16,80}... | collective-permute-start | bytes 196616 | tf_op jit(solution)/shard_map/ppermute | solution.py:25
  1.6 2.9 %collective-permute-done = bf16[4,8192]{1,0:T(4,128)(2,1)S(1)} collective-permute-done((bf16[4,8192]{1,0:T(4,128)(2,1)}, bf16[4,8192]{1,0:T(4,128)(2,1)S(1)}, u32[]{:S(2)}, u32[]{:S(2)}) %collective-permute-start) | collective-permute-done | bytes 65568 | tf_op jit(solution)/shard_map/ppermute | solution.py:25
  4.5 0.4 broadcast_in_dim.2
  4.9 23.9 %all_to_all.10.refs_0_ = bf16[16,4,8192]{2,1,0:T(4,128)(2,1)S(1)} all-to-all(bf16[16,4,8192]{2,1,0:T(4,128)(2,1)S(1)} %broadcast_in_dim.2), channel_id=1, replica_groups=mesh['xl'=2,'y'=4,'z'=4,'c'=2,'xh'=2] {'y','z'}, dimensions={0} | all-to-all | bytes 2097152 | tf_op jit(solution)/shard_map/all_to_all | solution.py:95
  28.8 0.0 collective-permute-start.6
  28.8 0.4 fusion
  29.2 2.8 %collective-permute-start.2 = (bf16[8,4,8192]{2,1,0:T(4,128)(2,1)S(1)}, bf16[8,4,8192]{2,1,0:T(4,128)(2,1)S(1)}, u32[]{:S(2)}, u32[]{:S(2)}) collective-permute-start(bf16[8,4,8192]{2,1,0:T(4,128)(2,1)S(1)} %get-tuple-element.9), channel_id=1, source_target_pairs={{0,65},{2,67},{4,69},{6,71},{8,73},{10,75},{12,77},{14,79},{16,81}... | collective-permute-start | bytes 1572872 | tf_op jit(solution)/shard_map/ppermute | solution.py:25
  32.0 0.2 collective-permute-start.1
  32.3 12.6 %collective-permute-done.2.refs_1_ = bf16[8,4,8192]{2,1,0:T(4,128)(2,1)S(1)} collective-permute-done((bf16[8,4,8192]{2,1,0:T(4,128)(2,1)S(1)}, bf16[8,4,8192]{2,1,0:T(4,128)(2,1)S(1)}, u32[]{:S(2)}, u32[]{:S(2)}) %collective-permute-start.2) | collective-permute-done | bytes 524320 | tf_op jit(solution)/shard_map/ppermute | solution.py:25
  44.8 1.3 %collective-permute-done.1.refs_0_ = bf16[8,4,8192]{2,1,0:T(4,128)(2,1)S(1)} collective-permute-done((bf16[8,4,8192]{2,1,0:T(4,128)(2,1)S(1)}, bf16[8,4,8192]{2,1,0:T(4,128)(2,1)S(1)}, u32[]{:S(2)}, u32[]{:S(2)}) %collective-permute-start.1) | collective-permute-done | bytes 524320 | tf_op jit(solution)/shard_map/ppermute | solution.py:25
  46.1 0.0 collective-permute-start.3
  46.1 0.0 collective-permute-done.6.refs_1_
  46.1 0.0 copy-start.2
  46.1 2.1 %copy-done.2 = bf16[231,8192]{1,0:T(8,128)(2,1)S(1)} copy-done((bf16[231,8192]{1,0:T(8,128)(2,1)S(1)}, bf16[231,8192]{1,0:T(8,128)(2,1)}, u32[]{:S(2)}) %copy-start.2) | copy-done | bytes 3784728
  48.2 2.7 %shard_map.48.refs_0_ = bf16[128,231]{1,0:T(8,128)(2,1)S(1)} custom-call(bf16[16,4,8192]{2,1,0:T(4,128)(2,1)S(1)} %all_to_all.10.refs_0_, bf16[16,4,8192]{2,1,0:T(4,128)(2,1)S(1)} %collective-permute-done.6.refs_1_, bf16[231,8192]{1,0:T(8,128)(2,1)S(1)} %copy-done.1, bf16[231,8192]{1,0:T(8,128)(2,1)S(1)} %copy-done.2), custom_call_target="tpu_custom_call" | custom-call | tf_op jit(solution)/shard_map/pallas_call | solution.py:77
  51.0 0.0 copy-start.3
  51.0 0.8 shard_map.49
  51.8 0.6 collective-permute-start.7
  52.4 0.0 collective-permute-done.4.refs_3_
  52.4 0.0 collective-permute-done.3.refs_2_
  52.4 0.6 copy-done.3
  53.0 2.7 %shard_map.46.refs_0_ = bf16[128,231]{1,0:T(8,128)(2,1)S(1)} custom-call(bf16[8,4,8192]{2,1,0:T(4,128)(2,1)S(1)} %collective-permute-done.1.refs_0_, bf16[8,4,8192]{2,1,0:T(4,128)(2,1)S(1)} %collective-permute-done.2.refs_1_, bf16[8,4,8192]{2,1,0:T(4,128)(2,1)S(1)} %collective-permute-done.3.refs_2_, bf16[8,4,8192]{2,1,0:T(4,128)(2,1)S(1)} %collective-permute-done.4.refs_3_, ...), custom_call_target="tpu_custom_call" | custom-call | tf_op jit(solution)/shard_map/pallas_call | solution.py:77
  55.8 0.8 shard_map.47
  56.6 0.6 collective-permute-start.5
  57.2 1.0 shard_map.50
  58.2 0.4 collective-permute-start.8
  58.6 1.3 %collective-permute-start.9 = (bf16[16,2,8192]{2,1,0:T(2,128)(2,1)S(1)}, bf16[16,2,8192]{2,1,0:T(2,128)(2,1)S(1)}, u32[]{:S(2)}, u32[]{:S(2)}) collective-permute-start(bf16[16,2,8192]{2,1,0:T(2,128)(2,1)S(1)} %get-tuple-element.8), channel_id=1, source_target_pairs={{0,65},{2,67},{4,69},{6,71},{8,73},{10,75},{12,77},{14,79},{16,81}... | collective-permute-start | bytes 1572872 | tf_op jit(solution)/shard_map/ppermute | solution.py:25
  59.9 12.2 %collective-permute-done.8.refs_3_ = bf16[16,2,8192]{2,1,0:T(2,128)(2,1)S(1)} collective-permute-done((bf16[16,2,8192]{2,1,0:T(2,128)(2,1)S(1)}, bf16[16,2,8192]{2,1,0:T(2,128)(2,1)S(1)}, u32[]{:S(2)}, u32[]{:S(2)}) %collective-permute-start.8) | collective-permute-done | bytes 524320 | tf_op jit(solution)/shard_map/ppermute | solution.py:25
  72.1 1.3 %collective-permute-done.9.refs_4_ = bf16[16,2,8192]{2,1,0:T(2,128)(2,1)S(1)} collective-permute-done((bf16[16,2,8192]{2,1,0:T(2,128)(2,1)S(1)}, bf16[16,2,8192]{2,1,0:T(2,128)(2,1)S(1)}, u32[]{:S(2)}, u32[]{:S(2)}) %collective-permute-start.9) | collective-permute-done | bytes 524320 | tf_op jit(solution)/shard_map/ppermute | solution.py:25
  73.4 1.3 %shard_map.51 = bf16[32,2,8192]{2,1,0:T(2,128)(2,1)S(1)} custom-call(bf16[128,231]{1,0:T(8,128)(2,1)S(1)} %shard_map.46.refs_0_, bf16[231,8192]{1,0:T(8,128)(2,1)S(1)} %copy-done, bf16[32,2,8192]{2,1,0:T(2,128)(2,1)S(1)} %collective-permute-done.5.refs_2_, bf16[16,2,8192]{2,1,0:T(2,128)(2,1)S(1)} %collective-permute-done.8.refs_3_, ...), custom_call_target="tpu_custom_call" | custom-call | tf_op jit(solution)/shard_map/pallas_call | solution.py:77
  74.7 23.7 %all_to_all.11 = bf16[32,2,8192]{2,1,0:T(2,128)(2,1)S(1)} all-to-all(bf16[32,2,8192]{2,1,0:T(2,128)(2,1)S(1)} %shard_map.51), channel_id=1, replica_groups=mesh['xl'=2,'y'=4,'z'=4,'c'=2,'xh'=2] {'y','z','xh'}, dimensions={0} | all-to-all | bytes 2097152 | tf_op jit(solution)/shard_map/all_to_all | solution.py:124
  98.4 1.6 %reduce_sum.12 = bf16[2,8192]{1,0:T(2,128)(2,1)} reduce(bf16[32,2,8192]{2,1,0:T(2,128)(2,1)S(1)} %all_to_all.11, bf16[]{:T(256)} %constant.2.clone.1), dimensions={0}, to_apply=%region_0.0 | reduce | flops 507904 | bytes 1081346 | tf_op jit(solution)/shard_map/reduce_sum | solution.py:125
  (7 shorter events, 0.0 us)
Async XLA Ops:
  0.0 46.1 %copy-start.1 = (bf16[231,8192]{1,0:T(8,128)(2,1)S(1)}, bf16[231,8192]{1,0:T(8,128)(2,1)}, u32[]{:S(2)}) copy-start(bf16[231,8192]{1,0:T(8,128)(2,1)} %refs_2_.1) | copy-start | bytes 11354116
  0.0 4.5 %collective-permute-start = (bf16[4,8192]{1,0:T(4,128)(2,1)}, bf16[4,8192]{1,0:T(4,128)(2,1)S(1)}, u32[]{:S(2)}, u32[]{:S(2)}) collective-permute-start(bf16[4,8192]{1,0:T(4,128)(2,1)} %param.4), channel_id=1, source_target_pairs={{0,64},{2,66},{4,68},{6,70},{8,72},{10,74},{12,76},{14,78},{16,80}... | collective-permute-start | bytes 196616 | tf_op jit(solution)/shard_map/ppermute | solution.py:25
  28.8 17.3 %collective-permute-start.6 = (bf16[16,4,8192]{2,1,0:T(4,128)(2,1)S(1)}, bf16[16,4,8192]{2,1,0:T(4,128)(2,1)S(1)}, u32[]{:S(2)}, u32[]{:S(2)}) collective-permute-start(bf16[16,4,8192]{2,1,0:T(4,128)(2,1)S(1)} %all_to_all.10.refs_0_), channel_id=1, source_target_pairs={{0,2},{2,0},{4,6},{6,4},{8,10},{10,8},{12,14},{14,12},{16,18},{18,... | collective-permute-start | bytes 3145736 | tf_op jit(solution)/shard_map/ppermute | solution.py:25
  29.2 15.6 %collective-permute-start.2 = (bf16[8,4,8192]{2,1,0:T(4,128)(2,1)S(1)}, bf16[8,4,8192]{2,1,0:T(4,128)(2,1)S(1)}, u32[]{:S(2)}, u32[]{:S(2)}) collective-permute-start(bf16[8,4,8192]{2,1,0:T(4,128)(2,1)S(1)} %get-tuple-element.9), channel_id=1, source_target_pairs={{0,65},{2,67},{4,69},{6,71},{8,73},{10,75},{12,77},{14,79},{16,81}... | collective-permute-start | bytes 1572872 | tf_op jit(solution)/shard_map/ppermute | solution.py:25
  32.0 18.9 %copy-start = (bf16[231,8192]{1,0:T(8,128)(2,1)S(1)}, bf16[231,8192]{1,0:T(8,128)(2,1)}, u32[]{:S(2)}) copy-start(bf16[231,8192]{1,0:T(8,128)(2,1)} %refs_1_.7) | copy-start | bytes 11354116
  32.0 14.1 %collective-permute-start.1 = (bf16[8,4,8192]{2,1,0:T(4,128)(2,1)S(1)}, bf16[8,4,8192]{2,1,0:T(4,128)(2,1)S(1)}, u32[]{:S(2)}, u32[]{:S(2)}) collective-permute-start(bf16[8,4,8192]{2,1,0:T(4,128)(2,1)S(1)} %get-tuple-element.10), channel_id=1, source_target_pairs={{0,64},{2,66},{4,68},{6,70},{8,72},{10,74},{12,76},{14,78},{16,80}... | collective-permute-start | bytes 1572872 | tf_op jit(solution)/shard_map/ppermute | solution.py:25
  44.8 7.6 %collective-permute-start.4 = (bf16[8,4,8192]{2,1,0:T(4,128)(2,1)S(1)}, bf16[8,4,8192]{2,1,0:T(4,128)(2,1)S(1)}, u32[]{:S(2)}, u32[]{:S(2)}) collective-permute-start(bf16[8,4,8192]{2,1,0:T(4,128)(2,1)S(1)} %collective-permute-done.2.refs_1_), channel_id=1, source_target_pairs={{0,2},{2,0},{4,6},{6,4},{8,10},{10,8},{12,14},{14,12},{16,18},{18,... | collective-permute-start | bytes 1572872 | tf_op jit(solution)/shard_map/ppermute | solution.py:25
  46.1 6.3 %collective-permute-start.3 = (bf16[8,4,8192]{2,1,0:T(4,128)(2,1)S(1)}, bf16[8,4,8192]{2,1,0:T(4,128)(2,1)S(1)}, u32[]{:S(2)}, u32[]{:S(2)}) collective-permute-start(bf16[8,4,8192]{2,1,0:T(4,128)(2,1)S(1)} %collective-permute-done.1.refs_0_), channel_id=1, source_target_pairs={{0,2},{2,0},{4,6},{6,4},{8,10},{10,8},{12,14},{14,12},{16,18},{18,... | collective-permute-start | bytes 1572872 | tf_op jit(solution)/shard_map/ppermute | solution.py:25
  46.1 2.1 %copy-start.2 = (bf16[231,8192]{1,0:T(8,128)(2,1)S(1)}, bf16[231,8192]{1,0:T(8,128)(2,1)}, u32[]{:S(2)}) copy-start(bf16[231,8192]{1,0:T(8,128)(2,1)} %refs_3_.1) | copy-start | bytes 11354116
  51.0 2.1 %copy-start.3 = (bf16[231,8192]{1,0:T(8,128)(2,1)S(1)}, bf16[231,8192]{1,0:T(8,128)(2,1)}, u32[]{:S(2)}) copy-start(bf16[231,8192]{1,0:T(8,128)(2,1)} %refs_3_.1) | copy-start | bytes 11354116
  51.8 5.4 %collective-permute-start.7 = (bf16[32,2,8192]{2,1,0:T(2,128)(2,1)S(1)}, bf16[32,2,8192]{2,1,0:T(2,128)(2,1)S(1)}, u32[]{:S(2)}, u32[]{:S(2)}) collective-permute-start(bf16[32,2,8192]{2,1,0:T(2,128)(2,1)S(1)} %shard_map.49), channel_id=1, source_target_pairs={{0,2},{2,0},{4,6},{6,4},{8,10},{10,8},{12,14},{14,12},{16,18},{18,... | collective-permute-start | bytes 3145736 | tf_op jit(solution)/shard_map/ppermute | solution.py:25
  56.6 3.3 %collective-permute-start.5 = (bf16[32,2,8192]{2,1,0:T(2,128)(2,1)S(1)}, bf16[32,2,8192]{2,1,0:T(2,128)(2,1)S(1)}, u32[]{:S(2)}, u32[]{:S(2)}) collective-permute-start(bf16[32,2,8192]{2,1,0:T(2,128)(2,1)S(1)} %shard_map.47), channel_id=1, source_target_pairs={{0,2},{2,0},{4,6},{6,4},{8,10},{10,8},{12,14},{14,12},{16,18},{18,... | collective-permute-start | bytes 3145736 | tf_op jit(solution)/shard_map/ppermute | solution.py:25
  58.2 13.9 %collective-permute-start.8 = (bf16[16,2,8192]{2,1,0:T(2,128)(2,1)S(1)}, bf16[16,2,8192]{2,1,0:T(2,128)(2,1)S(1)}, u32[]{:S(2)}, u32[]{:S(2)}) collective-permute-start(bf16[16,2,8192]{2,1,0:T(2,128)(2,1)S(1)} %get-tuple-element.7), channel_id=1, source_target_pairs={{0,64},{2,66},{4,68},{6,70},{8,72},{10,74},{12,76},{14,78},{16,80}... | collective-permute-start | bytes 1572872 | tf_op jit(solution)/shard_map/ppermute | solution.py:25
  58.6 14.9 %collective-permute-start.9 = (bf16[16,2,8192]{2,1,0:T(2,128)(2,1)S(1)}, bf16[16,2,8192]{2,1,0:T(2,128)(2,1)S(1)}, u32[]{:S(2)}, u32[]{:S(2)}) collective-permute-start(bf16[16,2,8192]{2,1,0:T(2,128)(2,1)S(1)} %get-tuple-element.8), channel_id=1, source_target_pairs={{0,65},{2,67},{4,69},{6,71},{8,73},{10,75},{12,77},{14,79},{16,81}... | collective-permute-start | bytes 1572872 | tf_op jit(solution)/shard_map/ppermute | solution.py:25

commit v4 on v3

v4 whole, which is shorter than its diff:
```python
import jax
import jax.numpy as jnp
from jax import lax
from jax.experimental import pallas as pl
from jax.experimental.pallas import tpu as pltpu
from jax.sharding import PartitionSpec as P


ALL = ("blk", "tensor")
BF = jnp.bfloat16
F32 = jnp.float32
R4 = range(4)


def flat(x, y, z, c):
    return ((x % 2 * 4 + y) * 4 + z) * 4 + c * 2 + x // 2


def move(v, to):
    pairs = [
        (flat(x, y, z, c), flat(*to(x, y, z, c)))
        for x in R4
        for y in R4
        for z in R4
        for c in range(2)
    ]
    return lax.ppermute(v, ALL, pairs)


def core(v):
    return move(v, lambda x, y, z, c: (x, y, z, 1 - c))


def ring(v, k):
    return move(
        v,
        lambda x, y, z, c: (x, (y + k) % 4, z, c) if c else (x, y, (z + k) % 4, c),
    )


def near_groups():
    return [
        [
            flat(h * 2 + l, m if c == 0 else s, s if c == 0 else m, c)
            for l in range(2)
            for m in R4
        ]
        for c in range(2)
        for h in range(2)
        for s in R4
    ]


def plane_groups():
    return [
        [
            flat(h * 2 + l, m if c == 0 else s, s if c == 0 else m, c)
            for l in range(2)
            for m in R4
            for h in range(2)
        ]
        for c in range(2)
        for s in R4
    ]


def rows_of(left, weight):
    return lax.dot_general(
        left, weight, (((1,), (1,)), ((), ())), preferred_element_type=F32
    )


def hidden_kernel(*refs):
    *x_refs, gate_ref, up_ref, hidden_ref = refs
    d = x_refs[0].shape[2]
    x = jnp.concatenate([r[...].reshape(-1, d) for r in x_refs], axis=0)
    gate = rows_of(x, gate_ref[...])
    up = rows_of(x, up_ref[...])
    hidden_ref[...] = (gate / (1.0 + jnp.exp(-gate)) * up).astype(BF)


def down_kernel(at, n_out, *refs):
    hidden_ref, down_ref, *more = refs[:-n_out]
    outs = refs[-n_out:]
    rows = sum(o.shape[0] for o in outs) * 2
    part = jnp.dot(
        hidden_ref[at : at + rows, :], down_ref[...], preferred_element_type=F32
    )
    for r in more:
        part += r[...].reshape(part.shape).astype(F32)
    each = rows // n_out
    for i, o in enumerate(outs):
        o[...] = part[i * each : (i + 1) * each].astype(BF).reshape(o.shape)


def add_one_kernel(
    hidden_ref, down_ref, fold_ref, lent_low_ref, lent_high_ref, low_ref, high_ref
):
    rows = hidden_ref.shape[0] // 2
    part = jnp.dot(
        hidden_ref[0:rows, :], down_ref[...], preferred_element_type=F32
    ) + fold_ref[...].reshape(rows, -1).astype(F32)
    each = rows // 2
    half = each // 2
    low, high = part[:each], part[each:]
    low_first = low[:half] + lent_low_ref[...].reshape(half, -1).astype(F32)
    high_last = high[half:] + lent_high_ref[...].reshape(half, -1).astype(F32)
    n = low_ref.shape[0] // 2
    low_ref[0:n] = low_first.astype(BF).reshape(n, 2, -1)
    low_ref[n:] = low[half:].astype(BF).reshape(n, 2, -1)
    high_ref[0:n] = high[:half].astype(BF).reshape(n, 2, -1)
    high_ref[n:] = high_last.astype(BF).reshape(n, 2, -1)


VM = pl.BlockSpec(memory_space=pltpu.VMEM)


def call(kernel, shapes, *args):
    return pl.pallas_call(
        kernel,
        out_shape=[jax.ShapeDtypeStruct(shape, BF) for shape in shapes],
        in_specs=[VM] * len(args),
        out_specs=[VM] * len(shapes),
        compiler_params=pltpu.CompilerParams(vmem_limit_bytes=20 * 2**20),
    )(*args)


def touch_kernel(*refs):
    *weights, out = refs
    out[...] = sum(w[0:8, 0:128].astype(F32) for w in weights)


def touch(*weights):
    return pl.pallas_call(
        touch_kernel,
        out_shape=jax.ShapeDtypeStruct((8, 128), F32),
        in_specs=[VM] * len(weights),
        out_specs=VM,
        compiler_params=pltpu.CompilerParams(
            vmem_limit_bytes=20 * 2**20, has_side_effects=True
        ),
    )(*weights)


def down(at, shapes, *args):
    return call(lambda *refs: down_kernel(at, len(shapes), *refs), shapes, *args)


def per_device(tokens, gate_weight, up_weight, down_weight):
    rows, d = tokens.shape
    f = gate_weight.shape[0]
    block = ring(tokens, 2)
    touch(gate_weight, up_weight)
    two = lax.all_to_all(
        jnp.broadcast_to(block[None], (8, rows, d)),
        ALL,
        0,
        0,
        axis_index_groups=near_groups(),
        tiled=True,
    )
    two_sib = core(two)
    low = ring(two, 1)
    high = ring(two, -1)
    (hidden,) = call(hidden_kernel, [(64, f)], two, two_sib, gate_weight, up_weight)
    (part,) = down(32, [(16, 2, d)], hidden, down_weight)
    part = core(part)
    part_a, part_b = down(0, [(8, 2, d)] * 2, hidden, down_weight, part)
    lent_low = ring(part_a, 1)
    lent_high = ring(part_b, -1)

    low_sib = core(low)
    high_sib = core(high)
    own_a = ring(low[:4], 1)
    own_b = ring(high[4:], -1)
    (hidden,) = call(
        hidden_kernel,
        [(128, f)],
        low,
        high,
        low_sib,
        high_sib,
        gate_weight,
        up_weight,
    )
    (part,) = down(64, [(32, 2, d)], hidden, down_weight)
    part = core(part)
    part_low, part_high = call(
        add_one_kernel,
        [(16, 2, d)] * 2,
        hidden,
        down_weight,
        part,
        lent_low,
        lent_high,
    )
    back_low = ring(part_low, 1)
    back_high = ring(part_high, -1)

    sib_a = core(own_a)
    sib_b = core(own_b)
    (hidden,) = call(
        hidden_kernel,
        [(64, f)],
        own_a,
        own_b,
        sib_a,
        sib_b,
        gate_weight,
        up_weight,
    )
    (part,) = down(32, [(16, 2, d)], hidden, down_weight)
    part = core(part)
    (part,) = down(
        0, [(16, 2, d)], hidden, down_weight, part, back_low, back_high
    )
    pieces = lax.all_to_all(
        part, ALL, 0, 0, axis_index_groups=plane_groups(), tiled=True
    )
    return jnp.sum(pieces.astype(F32), axis=0).astype(BF)


def solution(mesh):
    return jax.shard_map(
        per_device,
        mesh=mesh,
        in_specs=(P("blk", None), P(ALL, None), P(ALL, None), P(ALL, None)),
        out_specs=P(ALL, None),
        check_vma=False,
    )
```

time: 100 us -> 95.6 us (0.956)
  blocking collectives: 47.6 us -> 14.8 us
  starting transfers between devices: 7.52 us -> 21.4 us
  local copies, waits for them, and re-layouts: 3.5 us -> 9.63 us
  Pallas kernels: 9.43 us -> 14.7 us
  waiting for transfers between devices: 30.3 us -> 33.5 us
    all_to_all x2 -> x1, blocking collectives: 47.6 us -> 14.8 us  [per_device(): lax.all_to_all(jnp.broadcast_to(block[None], (8, rows, d)), ALL, 0, 0, ax...]
    ppermute x10 -> x17, starting transfers between devices: 7.52 us -> 16.6 us  [move(): return lax.ppermute(v, ALL, pairs)]
    unnamed x8 -> x12, local copies, waits for them, and re-layouts: 2.71 us -> 9.3 us
    all_to_all x0 -> x1, waiting for transfers between devices: none -> 4.93 us  [per_device(): lax.all_to_all(part, ALL, 0, 0, axis_index_groups=plane_groups(), tiled=T...]
    all_to_all x0 -> x1, starting transfers between devices: none -> 4.77 us  [per_device(): lax.all_to_all(part, ALL, 0, 0, axis_index_groups=plane_groups(), tiled=T...]
    pallas_call x6 -> x9, Pallas kernels: 9.43 us -> 14.1 us  [call(): pl.pallas_call(kernel, out_shape=[jax.ShapeDtypeStruct(shape, BF) for sha...]
    ppermute x10 -> x17, waiting for transfers between devices: 30.3 us -> 28.5 us  [move(): return lax.ppermute(v, ALL, pairs)]
  transfers between devices with their start and end apart: 10 -> 18, of which waited for: 5 -> 9; matrix products, arithmetic and copies ran while one was open for 0% -> 0% of each run, Pallas kernels for 8% -> 13%
where the time goes in v4:
time: 95.6 us; the launch traced here: 95.1 us
  waiting for transfers between devices  33.5 us (35%)
  starting transfers between devices  21.4 us (22%)
  blocking collectives  14.8 us (15%)
  Pallas kernels  14.7 us (15%)
  local copies, waits for them, and re-layouts  9.63 us (10%)
  other arithmetic  1.07 us (1%)
    ppermute x17, waiting for transfers between devices, move(): return lax.ppermute(v, ALL, pairs)  28.5 us
    ppermute x17, starting transfers between devices, move(): return lax.ppermute(v, ALL, pairs)  16.6 us
    all_to_all x1, blocking collectives, per_device(): lax.all_to_all(jnp.broadcast_to(block[None], (8, rows, d)), ALL, 0, 0, ax...  14.8 us
    pallas_call x9, Pallas kernels, call(): pl.pallas_call(kernel, out_shape=[jax.ShapeDtypeStruct(shape, BF) for sha...  14.1 us
    unnamed x12, local copies, waits for them, and re-layouts  9.3 us
    all_to_all x1, waiting for transfers between devices, per_device(): lax.all_to_all(part, ALL, 0, 0, axis_index_groups=plane_groups(), tiled=T...  4.93 us
    all_to_all x1, starting transfers between devices, per_device(): lax.all_to_all(part, ALL, 0, 0, axis_index_groups=plane_groups(), tiled=T...  4.77 us
  transfers between devices with their start and end apart: 18, of which 9 were waited for; matrix products, arithmetic and copies ran while one was open for 0% of the time, Pallas kernels for 13%

profile of v4, /device:TPU:0, one launch (start us, length us, event | category | flops | bytes accessed | tf_op | source)
XLA Modules:
  0.0 95.1 jit_solution(1797410997582384711)
XLA Ops:
  0.0 4.0 %collective-permute-start = (bf16[4,8192]{1,0:T(4,128)(2,1)}, bf16[4,8192]{1,0:T(4,128)(2,1)S(1)}, u32[]{:S(2)}, u32[]{:S(2)}) collective-permute-start(bf16[4,8192]{1,0:T(4,128)(2,1)} %param.4), channel_id=1, source_target_pairs={{0,8},{2,34},{4,12},{6,38},{8,0},{10,42},{12,4},{14,46},{16,24},{1... | collective-permute-start | bytes 196616 | tf_op jit(solution)/shard_map/ppermute | solution.py:27
  4.0 2.5 %collective-permute-done = bf16[4,8192]{1,0:T(4,128)(2,1)S(1)} collective-permute-done((bf16[4,8192]{1,0:T(4,128)(2,1)}, bf16[4,8192]{1,0:T(4,128)(2,1)S(1)}, u32[]{:S(2)}, u32[]{:S(2)}) %collective-permute-start) | collective-permute-done | bytes 65568 | tf_op jit(solution)/shard_map/ppermute | solution.py:27
  6.6 14.8 %all_to_all.10.refs_0_ = bf16[8,4,8192]{2,1,0:T(4,128)(2,1)S(1)} all-to-all(bf16[8,4,8192]{2,1,0:T(4,128)(2,1)S(1)} %broadcast_in_dim.2), channel_id=1, replica_groups={{0,16,32,48,64,80,96,112},{4,20,36,52,68,84,100,116},{8,24,40,56,72,88,..., dimensions={0} | all-to-all | bytes 1048576 | tf_op jit(solution)/shard_map/all_to_all | solution.py:154
  21.4 2.7 %collective-permute-start.3 = (bf16[8,4,8192]{2,1,0:T(4,128)(2,1)S(1)}, bf16[8,4,8192]{2,1,0:T(4,128)(2,1)S(1)}, u32[]{:S(2)}, u32[]{:S(2)}) collective-permute-start(bf16[8,4,8192]{2,1,0:T(4,128)(2,1)S(1)} %all_to_all.10.refs_0_), channel_id=1, source_target_pairs={{0,12},{2,50},{4,0},{6,54},{8,4},{10,58},{12,8},{14,62},{16,28},{1... | collective-permute-start | bytes 1572872 | tf_op jit(solution)/shard_map/ppermute | solution.py:27
  24.1 6.7 %collective-permute-done.3.refs_1_ = bf16[8,4,8192]{2,1,0:T(4,128)(2,1)S(1)} collective-permute-done((bf16[8,4,8192]{2,1,0:T(4,128)(2,1)S(1)}, bf16[8,4,8192]{2,1,0:T(4,128)(2,1)S(1)}, u32[]{:S(2)}, u32[]{:S(2)}) %collective-permute-start.3) | collective-permute-done | bytes 524320 | tf_op jit(solution)/shard_map/ppermute | solution.py:27
  30.8 3.7 %collective-permute-done.1.refs_0_ = bf16[8,4,8192]{2,1,0:T(4,128)(2,1)S(1)} collective-permute-done((bf16[8,4,8192]{2,1,0:T(4,128)(2,1)S(1)}, bf16[8,4,8192]{2,1,0:T(4,128)(2,1)S(1)}, u32[]{:S(2)}, u32[]{:S(2)}) %collective-permute-start.1) | collective-permute-done | bytes 524320 | tf_op jit(solution)/shard_map/ppermute | solution.py:27
  35.0 1.4 %collective-permute-done.8.refs_2_ = bf16[8,4,8192]{2,1,0:T(4,128)(2,1)S(1)} collective-permute-done((bf16[8,4,8192]{2,1,0:T(4,128)(2,1)S(1)}, bf16[8,4,8192]{2,1,0:T(4,128)(2,1)S(1)}, u32[]{:S(2)}, u32[]{:S(2)}) %collective-permute-start.8) | collective-permute-done | bytes 524320 | tf_op jit(solution)/shard_map/ppermute | solution.py:27
  36.4 2.1 %copy-done.1 = bf16[231,8192]{1,0:T(8,128)(2,1)S(1)} copy-done((bf16[231,8192]{1,0:T(8,128)(2,1)S(1)}, bf16[231,8192]{1,0:T(8,128)(2,1)}, u32[]{:S(2)}) %copy-start.1) | copy-done | bytes 3784728
  38.5 2.1 %copy-done.3 = bf16[231,8192]{1,0:T(8,128)(2,1)S(1)} copy-done((bf16[231,8192]{1,0:T(8,128)(2,1)S(1)}, bf16[231,8192]{1,0:T(8,128)(2,1)}, u32[]{:S(2)}) %copy-start.3) | copy-done | bytes 3784728
  40.6 2.7 %shard_map.49.refs_0_.hidden_ref = bf16[128,231]{1,0:T(8,128)(2,1)S(1)} custom-call(bf16[8,4,8192]{2,1,0:T(4,128)(2,1)S(1)} %collective-permute-done.1.refs_0_, bf16[8,4,8192]{2,1,0:T(4,128)(2,1)S(1)} %collective-permute-done.3.refs_1_, bf16[8,4,8192]{2,1,0:T(4,128)(2,1)S(1)} %collective-permute-done.8.refs_2_, ...), custom_call_target="tpu_custom_call" | custom-call | tf_op jit(solution)/shard_map/pallas_call | solution.py:119
  43.3 0.8 shard_map.50
  44.4 1.0 %copy-done.4 = bf16[231,8192]{1,0:T(8,128)(2,1)S(1)} copy-done((bf16[231,8192]{1,0:T(8,128)(2,1)S(1)}, bf16[231,8192]{1,0:T(8,128)(2,1)}, u32[]{:S(2)}) %copy-start.4) | copy-done | bytes 3784728
  45.4 2.5 %shard_map.51.refs_0_ = bf16[64,231]{1,0:T(8,128)(2,1)S(1)} custom-call(bf16[8,4,8192]{2,1,0:T(4,128)(2,1)S(1)} %all_to_all.10.refs_0_, bf16[8,4,8192]{2,1,0:T(4,128)(2,1)S(1)} %collective-permute-done.11.refs_1_, bf16[231,8192]{1,0:T(8,128)(2,1)S(1)} %copy-done.1, bf16[231,8192]{1,0:T(8,128)(2,1)S(1)} %copy-done.4), custom_call_target="tpu_custom_call" | custom-call | tf_op jit(solution)/shard_map/pallas_call | solution.py:119
  47.9 0.8 shard_map.52
  49.1 0.8 collective-permute-start.4
  50.0 1.3 %collective-permute-start.2 = (bf16[4,4,8192]{2,1,0:T(4,128)(2,1)S(1)}, bf16[4,4,8192]{2,1,0:T(4,128)(2,1)S(1)}, u32[]{:S(2)}, u32[]{:S(2)}) collective-permute-start(bf16[4,4,8192]{2,1,0:T(4,128)(2,1)S(1)} %slice.8), channel_id=1, source_target_pairs={{0,4},{2,18},{4,8},{6,22},{8,12},{10,26},{12,0},{14,30},{16,20},{1... | collective-permute-start | bytes 786440 | tf_op jit(solution)/shard_map/ppermute | solution.py:27
  51.3 4.2 %collective-permute-done.4.refs_1_ = bf16[4,4,8192]{2,1,0:T(4,128)(2,1)S(1)} collective-permute-done((bf16[4,4,8192]{2,1,0:T(4,128)(2,1)S(1)}, bf16[4,4,8192]{2,1,0:T(4,128)(2,1)S(1)}, u32[]{:S(2)}, u32[]{:S(2)}) %collective-permute-start.4) | collective-permute-done | bytes 262176 | tf_op jit(solution)/shard_map/ppermute | solution.py:27
  55.5 2.1 %collective-permute-done.2.refs_0_ = bf16[4,4,8192]{2,1,0:T(4,128)(2,1)S(1)} collective-permute-done((bf16[4,4,8192]{2,1,0:T(4,128)(2,1)S(1)}, bf16[4,4,8192]{2,1,0:T(4,128)(2,1)S(1)}, u32[]{:S(2)}, u32[]{:S(2)}) %collective-permute-start.2) | collective-permute-done | bytes 262176 | tf_op jit(solution)/shard_map/ppermute | solution.py:27
  57.6 0.8 shard_map.53
  58.6 3.2 %collective-permute-start.14 = (bf16[8,2,8192]{2,1,0:T(2,128)(2,1)S(1)}, bf16[8,2,8192]{2,1,0:T(2,128)(2,1)S(1)}, u32[]{:S(2)}, u32[]{:S(2)}) collective-permute-start(bf16[8,2,8192]{2,1,0:T(2,128)(2,1)S(1)} %get-tuple-element.10), channel_id=1, source_target_pairs={{0,12},{2,50},{4,0},{6,54},{8,4},{10,58},{12,8},{14,62},{16,28},{1... | collective-permute-start | bytes 786440 | tf_op jit(solution)/shard_map/ppermute | solution.py:27
  61.8 2.5 %shard_map.47.refs_0_ = bf16[64,231]{1,0:T(8,128)(2,1)S(1)} custom-call(bf16[4,4,8192]{2,1,0:T(4,128)(2,1)S(1)} %collective-permute-done.2.refs_0_, bf16[4,4,8192]{2,1,0:T(4,128)(2,1)S(1)} %collective-permute-done.4.refs_1_, bf16[4,4,8192]{2,1,0:T(4,128)(2,1)S(1)} %collective-permute-done.5.refs_2_, bf16[4,4,8192]{2,1,0:T(4,128)(2,1)S(1)} %collective-permute-done.6.refs_3_, ...), custom_call_target="tpu_custom_call" | custom-call | tf_op jit(solution)/shard_map/pallas_call | solution.py:119
  64.3 0.8 shard_map.48
  65.2 0.9 collective-permute-done.13.lent_low_ref
  66.1 1.1 %shard_map.54 = (bf16[16,2,8192]{2,1,0:T(2,128)(2,1)S(1)}, bf16[16,2,8192]{2,1,0:T(2,128)(2,1)S(1)}) custom-call(bf16[128,231]{1,0:T(8,128)(2,1)S(1)} %shard_map.49.refs_0_.hidden_ref, bf16[231,8192]{1,0:T(8,128)(2,1)S(1)} %copy-done, bf16[32,2,8192]{2,1,0:T(2,128)(2,1)S(1)} %collective-permute-done.10.fold_ref, ...), custom_call_target="tpu_custom_call" | custom-call | tf_op jit(solution)/shard_map/pallas_call | solution.py:119
  67.3 3.3 %collective-permute-start.16 = (bf16[16,2,8192]{2,1,0:T(2,128)(2,1)S(1)}, bf16[16,2,8192]{2,1,0:T(2,128)(2,1)S(1)}, u32[]{:S(2)}, u32[]{:S(2)}) collective-permute-start(bf16[16,2,8192]{2,1,0:T(2,128)(2,1)S(1)} %get-tuple-element.12), channel_id=1, source_target_pairs={{0,12},{2,50},{4,0},{6,54},{8,4},{10,58},{12,8},{14,62},{16,28},{1... | collective-permute-start | bytes 1572872 | tf_op jit(solution)/shard_map/ppermute | solution.py:27
  70.6 7.1 %collective-permute-done.15.refs_3_ = bf16[16,2,8192]{2,1,0:T(2,128)(2,1)S(1)} collective-permute-done((bf16[16,2,8192]{2,1,0:T(2,128)(2,1)S(1)}, bf16[16,2,8192]{2,1,0:T(2,128)(2,1)S(1)}, u32[]{:S(2)}, u32[]{:S(2)}) %collective-permute-start.15) | collective-permute-done | bytes 524320 | tf_op jit(solution)/shard_map/ppermute | solution.py:27
  77.7 1.9 %shard_map.55 = bf16[16,2,8192]{2,1,0:T(2,128)(2,1)} custom-call(bf16[64,231]{1,0:T(8,128)(2,1)S(1)} %shard_map.47.refs_0_, bf16[231,8192]{1,0:T(8,128)(2,1)S(1)} %copy-done, bf16[16,2,8192]{2,1,0:T(2,128)(2,1)S(1)} %collective-permute-done.7.refs_2_, bf16[16,2,8192]{2,1,0:T(2,128)(2,1)S(1)} %collective-permute-done.15.refs_3_, ...), custom_call_target="tpu_custom_call" | custom-call | tf_op jit(solution)/shard_map/pallas_call | solution.py:119
  79.6 4.8 %all-to-all-start.1 = ((bf16[16,2,8192]{2,1,0:T(2,128)(2,1)}), bf16[16,2,8192]{2,1,0:T(2,128)(2,1)S(1)}, u32[]{:S(2)}, u32[]{:S(2)}) async-start(bf16[16,2,8192]{2,1,0:T(2,128)(2,1)} %shard_map.55), calls=%async_computation.1 | async-start | bytes 1048576 | tf_op jit(solution)/shard_map/all_to_all | solution.py:217
  84.4 2.1 %copy-done.2 = bf16[231,8192]{1,0:T(8,128)(2,1)S(1)} copy-done((bf16[231,8192]{1,0:T(8,128)(2,1)S(1)}, bf16[231,8192]{1,0:T(8,128)(2,1)}, u32[]{:S(2)}) %copy-start.2) | copy-done | bytes 3784728
  86.5 2.1 %copy-done.5 = bf16[231,8192]{1,0:T(8,128)(2,1)S(1)} copy-done((bf16[231,8192]{1,0:T(8,128)(2,1)S(1)}, bf16[231,8192]{1,0:T(8,128)(2,1)}, u32[]{:S(2)}) %copy-start.5) | copy-done | bytes 3784728
  89.1 4.9 %all-to-all-done.1 = bf16[16,2,8192]{2,1,0:T(2,128)(2,1)S(1)} async-done(((bf16[16,2,8192]{2,1,0:T(2,128)(2,1)}), bf16[16,2,8192]{2,1,0:T(2,128)(2,1)S(1)}, u32[]{:S(2)}, u32[]{:S(2)}) %all-to-all-start.1) | async-done | bytes 524320 | tf_op jit(solution)/shard_map/all_to_all | solution.py:217
  94.1 1.1 %reduce_sum.12 = bf16[2,8192]{1,0:T(2,128)(2,1)} reduce(bf16[16,2,8192]{2,1,0:T(2,128)(2,1)S(1)} %all-to-all-done.1, bf16[]{:T(256)} %constant.2.clone.1), dimensions={0}, to_apply=%region_0.0 | reduce | flops 245760 | bytes 557058 | tf_op jit(solution)/shard_map/reduce_sum | solution.py:220
  (31 shorter events, 2.2 us)
Async XLA Ops:
  0.0 6.4 %collective-permute-start = (bf16[4,8192]{1,0:T(4,128)(2,1)}, bf16[4,8192]{1,0:T(4,128)(2,1)S(1)}, u32[]{:S(2)}, u32[]{:S(2)}) collective-permute-start(bf16[4,8192]{1,0:T(4,128)(2,1)} %param.4), channel_id=1, source_target_pairs={{0,8},{2,34},{4,12},{6,38},{8,0},{10,42},{12,4},{14,46},{16,24},{1... | collective-permute-start | bytes 196616 | tf_op jit(solution)/shard_map/ppermute | solution.py:27
  21.4 21.9 %copy-start = (bf16[231,8192]{1,0:T(8,128)(2,1)S(1)}, bf16[231,8192]{1,0:T(8,128)(2,1)}, u32[]{:S(2)}) copy-start(bf16[231,8192]{1,0:T(8,128)(2,1)} %refs_1_.11) | copy-start | bytes 11354116
  21.4 9.4 %collective-permute-start.3 = (bf16[8,4,8192]{2,1,0:T(4,128)(2,1)S(1)}, bf16[8,4,8192]{2,1,0:T(4,128)(2,1)S(1)}, u32[]{:S(2)}, u32[]{:S(2)}) collective-permute-start(bf16[8,4,8192]{2,1,0:T(4,128)(2,1)S(1)} %all_to_all.10.refs_0_), channel_id=1, source_target_pairs={{0,12},{2,50},{4,0},{6,54},{8,4},{10,58},{12,8},{14,62},{16,28},{1... | collective-permute-start | bytes 1572872 | tf_op jit(solution)/shard_map/ppermute | solution.py:27
  24.1 10.4 %collective-permute-start.1 = (bf16[8,4,8192]{2,1,0:T(4,128)(2,1)S(1)}, bf16[8,4,8192]{2,1,0:T(4,128)(2,1)S(1)}, u32[]{:S(2)}, u32[]{:S(2)}) collective-permute-start(bf16[8,4,8192]{2,1,0:T(4,128)(2,1)S(1)} %all_to_all.10.refs_0_), channel_id=1, source_target_pairs={{0,4},{2,18},{4,8},{6,22},{8,12},{10,26},{12,0},{14,30},{16,20},{1... | collective-permute-start | bytes 1572872 | tf_op jit(solution)/shard_map/ppermute | solution.py:27
  30.8 4.2 %collective-permute-start.9 = (bf16[8,4,8192]{2,1,0:T(4,128)(2,1)S(1)}, bf16[8,4,8192]{2,1,0:T(4,128)(2,1)S(1)}, u32[]{:S(2)}, u32[]{:S(2)}) collective-permute-start(bf16[8,4,8192]{2,1,0:T(4,128)(2,1)S(1)} %collective-permute-done.3.refs_1_), channel_id=1, source_target_pairs={{0,2},{2,0},{4,6},{6,4},{8,10},{10,8},{12,14},{14,12},{16,18},{18,... | collective-permute-start | bytes 1572872 | tf_op jit(solution)/shard_map/ppermute | solution.py:27
  34.5 1.9 %collective-permute-start.8 = (bf16[8,4,8192]{2,1,0:T(4,128)(2,1)S(1)}, bf16[8,4,8192]{2,1,0:T(4,128)(2,1)S(1)}, u32[]{:S(2)}, u32[]{:S(2)}) collective-permute-start(bf16[8,4,8192]{2,1,0:T(4,128)(2,1)S(1)} %collective-permute-done.1.refs_0_), channel_id=1, source_target_pairs={{0,2},{2,0},{4,6},{6,4},{8,10},{10,8},{12,14},{14,12},{16,18},{18,... | collective-permute-start | bytes 1572872 | tf_op jit(solution)/shard_map/ppermute | solution.py:27
  34.5 9.9 %collective-permute-start.11 = (bf16[8,4,8192]{2,1,0:T(4,128)(2,1)S(1)}, bf16[8,4,8192]{2,1,0:T(4,128)(2,1)S(1)}, u32[]{:S(2)}, u32[]{:S(2)}) collective-permute-start(bf16[8,4,8192]{2,1,0:T(4,128)(2,1)S(1)} %all_to_all.10.refs_0_), channel_id=1, source_target_pairs={{0,2},{2,0},{4,6},{6,4},{8,10},{10,8},{12,14},{14,12},{16,18},{18,... | collective-permute-start | bytes 1572872 | tf_op jit(solution)/shard_map/ppermute | solution.py:27
  36.4 2.1 %copy-start.1 = (bf16[231,8192]{1,0:T(8,128)(2,1)S(1)}, bf16[231,8192]{1,0:T(8,128)(2,1)}, u32[]{:S(2)}) copy-start(bf16[231,8192]{1,0:T(8,128)(2,1)} %refs_2_.1) | copy-start | bytes 11354116
  38.5 2.1 %copy-start.3 = (bf16[231,8192]{1,0:T(8,128)(2,1)S(1)}, bf16[231,8192]{1,0:T(8,128)(2,1)}, u32[]{:S(2)}) copy-start(bf16[231,8192]{1,0:T(8,128)(2,1)} %refs_3_.1) | copy-start | bytes 11354116
  43.3 2.1 %copy-start.4 = (bf16[231,8192]{1,0:T(8,128)(2,1)S(1)}, bf16[231,8192]{1,0:T(8,128)(2,1)}, u32[]{:S(2)}) copy-start(bf16[231,8192]{1,0:T(8,128)(2,1)} %refs_3_.1) | copy-start | bytes 11354116
  44.2 21.9 %collective-permute-start.10 = (bf16[32,2,8192]{2,1,0:T(2,128)(2,1)S(1)}, bf16[32,2,8192]{2,1,0:T(2,128)(2,1)S(1)}, u32[]{:S(2)}, u32[]{:S(2)}) collective-permute-start(bf16[32,2,8192]{2,1,0:T(2,128)(2,1)S(1)} %shard_map.50), channel_id=1, source_target_pairs={{0,2},{2,0},{4,6},{6,4},{8,10},{10,8},{12,14},{14,12},{16,18},{18,... | collective-permute-start | bytes 3145736 | tf_op jit(solution)/shard_map/ppermute | solution.py:27
  48.8 8.9 %collective-permute-start.12 = (bf16[16,2,8192]{2,1,0:T(2,128)(2,1)S(1)}, bf16[16,2,8192]{2,1,0:T(2,128)(2,1)S(1)}, u32[]{:S(2)}, u32[]{:S(2)}) collective-permute-start(bf16[16,2,8192]{2,1,0:T(2,128)(2,1)S(1)} %shard_map.52), channel_id=1, source_target_pairs={{0,2},{2,0},{4,6},{6,4},{8,10},{10,8},{12,14},{14,12},{16,18},{18,... | collective-permute-start | bytes 1572872 | tf_op jit(solution)/shard_map/ppermute | solution.py:27
  49.1 6.4 %collective-permute-start.4 = (bf16[4,4,8192]{2,1,0:T(4,128)(2,1)S(1)}, bf16[4,4,8192]{2,1,0:T(4,128)(2,1)S(1)}, u32[]{:S(2)}, u32[]{:S(2)}) collective-permute-start(bf16[4,4,8192]{2,1,0:T(4,128)(2,1)S(1)} %slice.9), channel_id=1, source_target_pairs={{0,12},{2,50},{4,0},{6,54},{8,4},{10,58},{12,8},{14,62},{16,28},{1... | collective-permute-start | bytes 786440 | tf_op jit(solution)/shard_map/ppermute | solution.py:27
  50.0 7.7 %collective-permute-start.2 = (bf16[4,4,8192]{2,1,0:T(4,128)(2,1)S(1)}, bf16[4,4,8192]{2,1,0:T(4,128)(2,1)S(1)}, u32[]{:S(2)}, u32[]{:S(2)}) collective-permute-start(bf16[4,4,8192]{2,1,0:T(4,128)(2,1)S(1)} %slice.8), channel_id=1, source_target_pairs={{0,4},{2,18},{4,8},{6,22},{8,12},{10,26},{12,0},{14,30},{16,20},{1... | collective-permute-start | bytes 786440 | tf_op jit(solution)/shard_map/ppermute | solution.py:27
  55.5 6.3 %collective-permute-start.6 = (bf16[4,4,8192]{2,1,0:T(4,128)(2,1)S(1)}, bf16[4,4,8192]{2,1,0:T(4,128)(2,1)S(1)}, u32[]{:S(2)}, u32[]{:S(2)}) collective-permute-start(bf16[4,4,8192]{2,1,0:T(4,128)(2,1)S(1)} %collective-permute-done.4.refs_1_), channel_id=1, source_target_pairs={{0,2},{2,0},{4,6},{6,4},{8,10},{10,8},{12,14},{14,12},{16,18},{18,... | collective-permute-start | bytes 786440 | tf_op jit(solution)/shard_map/ppermute | solution.py:27
  57.6 4.1 %collective-permute-start.5 = (bf16[4,4,8192]{2,1,0:T(4,128)(2,1)S(1)}, bf16[4,4,8192]{2,1,0:T(4,128)(2,1)S(1)}, u32[]{:S(2)}, u32[]{:S(2)}) collective-permute-start(bf16[4,4,8192]{2,1,0:T(4,128)(2,1)S(1)} %collective-permute-done.2.refs_0_), channel_id=1, source_target_pairs={{0,2},{2,0},{4,6},{6,4},{8,10},{10,8},{12,14},{14,12},{16,18},{18,... | collective-permute-start | bytes 786440 | tf_op jit(solution)/shard_map/ppermute | solution.py:27
  58.5 7.7 %collective-permute-start.13 = (bf16[8,2,8192]{2,1,0:T(2,128)(2,1)S(1)}, bf16[8,2,8192]{2,1,0:T(2,128)(2,1)S(1)}, u32[]{:S(2)}, u32[]{:S(2)}) collective-permute-start(bf16[8,2,8192]{2,1,0:T(2,128)(2,1)S(1)} %get-tuple-element.9), channel_id=1, source_target_pairs={{0,4},{2,18},{4,8},{6,22},{8,12},{10,26},{12,0},{14,30},{16,20},{1... | collective-permute-start | bytes 786440 | tf_op jit(solution)/shard_map/ppermute | solution.py:27
  58.6 7.5 %collective-permute-start.14 = (bf16[8,2,8192]{2,1,0:T(2,128)(2,1)S(1)}, bf16[8,2,8192]{2,1,0:T(2,128)(2,1)S(1)}, u32[]{:S(2)}, u32[]{:S(2)}) collective-permute-start(bf16[8,2,8192]{2,1,0:T(2,128)(2,1)S(1)} %get-tuple-element.10), channel_id=1, source_target_pairs={{0,12},{2,50},{4,0},{6,54},{8,4},{10,58},{12,8},{14,62},{16,28},{1... | collective-permute-start | bytes 786440 | tf_op jit(solution)/shard_map/ppermute | solution.py:27
  65.1 5.5 %collective-permute-start.7 = (bf16[16,2,8192]{2,1,0:T(2,128)(2,1)S(1)}, bf16[16,2,8192]{2,1,0:T(2,128)(2,1)S(1)}, u32[]{:S(2)}, u32[]{:S(2)}) collective-permute-start(bf16[16,2,8192]{2,1,0:T(2,128)(2,1)S(1)} %shard_map.48), channel_id=1, source_target_pairs={{0,2},{2,0},{4,6},{6,4},{8,10},{10,8},{12,14},{14,12},{16,18},{18,... | collective-permute-start | bytes 1572872 | tf_op jit(solution)/shard_map/ppermute | solution.py:27
  67.3 10.5 %collective-permute-start.15 = (bf16[16,2,8192]{2,1,0:T(2,128)(2,1)S(1)}, bf16[16,2,8192]{2,1,0:T(2,128)(2,1)S(1)}, u32[]{:S(2)}, u32[]{:S(2)}) collective-permute-start(bf16[16,2,8192]{2,1,0:T(2,128)(2,1)S(1)} %get-tuple-element.11), channel_id=1, source_target_pairs={{0,4},{2,18},{4,8},{6,22},{8,12},{10,26},{12,0},{14,30},{16,20},{1... | collective-permute-start | bytes 1572872 | tf_op jit(solution)/shard_map/ppermute | solution.py:27
  67.3 10.4 %collective-permute-start.16 = (bf16[16,2,8192]{2,1,0:T(2,128)(2,1)S(1)}, bf16[16,2,8192]{2,1,0:T(2,128)(2,1)S(1)}, u32[]{:S(2)}, u32[]{:S(2)}) collective-permute-start(bf16[16,2,8192]{2,1,0:T(2,128)(2,1)S(1)} %get-tuple-element.12), channel_id=1, source_target_pairs={{0,12},{2,50},{4,0},{6,54},{8,4},{10,58},{12,8},{14,62},{16,28},{1... | collective-permute-start | bytes 1572872 | tf_op jit(solution)/shard_map/ppermute | solution.py:27
  79.6 14.5 %all-to-all-start.1 = ((bf16[16,2,8192]{2,1,0:T(2,128)(2,1)}), bf16[16,2,8192]{2,1,0:T(2,128)(2,1)S(1)}, u32[]{:S(2)}, u32[]{:S(2)}) async-start(bf16[16,2,8192]{2,1,0:T(2,128)(2,1)} %shard_map.55), calls=%async_computation.1 | async-start | bytes 1048576 | tf_op jit(solution)/shard_map/all_to_all | solution.py:217
  84.4 2.1 %copy-start.2 = (bf16[231,8192]{1,0:T(8,128)(2,1)S(1)}, bf16[231,8192]{1,0:T(8,128)(2,1)}, u32[]{:S(2)}) copy-start(bf16[231,8192]{1,0:T(8,128)(2,1)} %refs_2_.1) | copy-start | bytes 11354116
  86.5 2.1 %copy-start.5 = (bf16[231,8192]{1,0:T(8,128)(2,1)S(1)}, bf16[231,8192]{1,0:T(8,128)(2,1)}, u32[]{:S(2)}) copy-start(bf16[231,8192]{1,0:T(8,128)(2,1)} %refs_3_.1) | copy-start | bytes 11354116
